TPU v7x, 32 devices: a whole 2x2x4 slice. The times are simulated.
32 devices in a mesh: ctx: 16 (over z, x, core), fsdp: 2 (over y).
Axes of the slice: x: 2, y: 2, z: 4, core: 2. Of those that a mesh axis runs over, the one named last changes fastest.
Arguments:
- layer_input: bfloat16 [2048, 4096], P('ctx'), may hold values from -8 to 8
- gain: float32 [4096], replicated, may hold values from 0.5 to 1.5
- codes: int32 [4096, 384], P('fsdp'), may hold values from -2147483648 to 2147483646
- column_scale_quantized: int32 [64, 3072], P('fsdp'), may hold values from 0 to 255
- block_second_scale: float32 [64], replicated, may hold values from 0.03 to 0.12
- query_down_map: bfloat16 [4096, 16], replicated, may hold values from -0.09375 to 0.09375
- query_up_map: bfloat16 [16, 2048], P(None, 'fsdp'), may hold values from -0.29882812 to 0.29882812
- token_document: int32 [2048], P('ctx'), may hold values from 0 to 3, as said below
- output_cotangent: bfloat16 [2048, 2048], P('ctx', 'fsdp'), may hold values from -0.059814453 to 0.059814453
Outputs:
- attn: bfloat16 [2048, 2048], P('ctx', 'fsdp')
- grad_a: float32 [4096, 16], replicated
- up_map_gradient: float32 [16, 2048], P(None, 'fsdp')
Inputs may be any that keep to these rules, and one draw needn't show every extreme that they name: token_document never falls along the sequence; each document has 1 to 1536 tokens and one has exactly 1536.
All inputs are finite; a program needn't handle non-finite values.
Results may differ from a plain program's by a relative error of at most 0.028.
Values may be sent and summed in bfloat16 or wider, within the bound.
A program may use at most 192 MiB of HBM per device.

v0:
```python
import math
import functools

import jax
import jax.numpy as jnp
from jax import lax
from jax.experimental import pallas as pl
from jax.experimental.pallas import tpu as pltpu
from jax.sharding import PartitionSpec as P

QUERY_HEADS = 16
KEY_VALUE_HEADS = 4
HEAD_SIZE = 128
ADAPTER_SCALE = 2.0
ROPE_BASE = 500000.0
ID_ROWS = 16
MESH = pl.DeviceIdType.MESH
F32 = jnp.float32
BF16 = jnp.bfloat16

NF4_LEVELS = [
    -1.0,
    -0.6961928009986877,
    -0.5250730514526367,
    -0.39491748809814453,
    -0.28444138169288635,
    -0.18477343022823334,
    -0.09105003625154495,
    0.0,
    0.07958029955625534,
    0.16093020141124725,
    0.24611230194568634,
    0.33791524171829224,
    0.44070982933044434,
    0.5626170039176941,
    0.7229568362236023,
    1.0,
]


def take_lanes(values, index):
    return jnp.take_along_axis(values, index, axis=1, mode="promise_in_bounds")


def nt(a, b):
    return lax.dot_general(a, b, (((1,), (1,)), ((), ())), preferred_element_type=F32)


def tn(a, b):
    return lax.dot_general(a, b, (((0,), (0,)), ((), ())), preferred_element_type=F32)


def proj_kernel(
    x_ref, gain_ref, codes_ref, cs_ref, bss_ref, qdown_ref, qup_ref, ids_ref, cos_ref, sin_ref,
    q_ref, kv_ref, xn_ref, lr_ref,
    scl, vscl, acc, acct, own_kv, send_kv, recv_kv, send_q, recv_q, send_sem, recv_sem,
):
    member = lax.axis_index("fsdp")
    partner = 1 - member
    rows = x_ref.shape[0]
    width = x_ref.shape[1]
    depth = codes_ref.shape[0]
    blocks = cs_ref.shape[0]
    block_rows = depth // blocks
    half_lanes = 64

    barrier = pltpu.get_barrier_semaphore()
    pl.semaphore_signal(barrier, inc=1, device_id={"fsdp": partner}, device_id_type=MESH)
    pl.semaphore_wait(barrier, 1)

    lane = lax.broadcasted_iota(jnp.int32, (blocks, 128), 1)
    second = bss_ref[pl.ds(pl.multiple_of(member * blocks, 8), blocks), :]
    for tile in range(3):
        source = [
            (cs_ref[:, tile * 1024 + m * 128 : tile * 1024 + (m + 1) * 128].astype(F32) + 1.0)
            / 256.0
            * second
            for m in range(8)
        ]
        for n in range(8):
            index = 8 * (lane % 16) + n
            picked = take_lanes(source[0], index)
            for m in range(1, 8):
                picked = jnp.where(lane // 16 == m, take_lanes(source[m], index), picked)
            scl[tile * 8 + n] = picked

    for r in range(0, rows, 16):
        wide = x_ref[r : r + 16, :].astype(F32)
        inverse = lax.rsqrt(jnp.mean(wide * wide, axis=-1, keepdims=True) + 1e-05)
        xn_ref[r : r + 16, :] = (wide * inverse * gain_ref[...]).astype(BF16)
    lr_t = nt(qdown_ref[...], xn_ref[...]).astype(BF16)
    lr_ref[...] = lr_t

    level_lane = lax.broadcasted_iota(jnp.int32, (block_rows, 128), 1)
    table = jnp.zeros((block_rows, 128), F32)
    for code, level in enumerate(NF4_LEVELS):
        table = jnp.where(level_lane % 16 == code, F32(level), table)
    low_lanes = level_lane < half_lanes

    pr = lax.broadcasted_iota(jnp.int32, (128, 128), 0)
    pd = lax.broadcasted_iota(jnp.int32, (128, 128), 1)
    perm = (pd == 8 * (pr % 16) + pr // 16).astype(F32).astype(BF16)

    chunk = 512
    per_chunk = chunk // block_rows

    def phase(low_tile, high_tile):
        low_at = pl.multiple_of(low_tile * 128, 128)
        high_at = pl.multiple_of(high_tile * 128, 128)
        for n in range(8):
            vscl[n] = jnp.where(
                lane < half_lanes, scl[low_tile * 8 + n], scl[high_tile * 8 + n]
            )
        acc[...] = jnp.zeros_like(acc)

        def step(k, carry):
            lhs = xn_ref[:, pl.ds(pl.multiple_of(member * depth + k * chunk, 128), chunk)]
            words = []
            for b in range(per_chunk):
                at = pl.multiple_of(k * chunk + b * block_rows, block_rows)
                words.append(
                    jnp.where(
                        low_lanes,
                        codes_ref[pl.ds(at, block_rows), pl.ds(low_at, 128)],
                        codes_ref[pl.ds(at, block_rows), pl.ds(high_at, 128)],
                    )
                )
            for pair in range(4):
                planes = []
                for n in (2 * pair, 2 * pair + 1):
                    pieces = []
                    for b in range(per_chunk):
                        code = jnp.bitwise_and(jnp.right_shift(words[b], 4 * n), 15)
                        scale = vscl[n, pl.ds(k * per_chunk + b, 1), :]
                        pieces.append((take_lanes(table, code) * scale).astype(BF16))
                    planes.append(jnp.concatenate(pieces, axis=0))
                weight = jnp.concatenate(planes, axis=1)
                acc[:, pair * 256 : (pair + 1) * 256] += jnp.dot(
                    lhs, weight, preferred_element_type=F32
                )
            return carry

        lax.fori_loop(0, depth // chunk, step, 0)

    def turn(out):
        for n in range(8):
            out[n] = acc[:, n * 128 : (n + 1) * 128].T

    def exchange(src, dst, number):
        copy = pltpu.make_async_remote_copy(
            src_ref=src,
            dst_ref=dst,
            send_sem=send_sem.at[number],
            recv_sem=recv_sem.at[number],
            device_id={"fsdp": partner},
            device_id_type=MESH,
        )
        copy.start()
        return copy

    phase(1, 2)
    turn(acct)
    own_at = pl.multiple_of(member * 64, 64)
    other_at = pl.multiple_of(partner * 64, 64)
    send_kv[...] = acct[:, pl.ds(other_at, 64), :].astype(BF16)
    copy_kv = exchange(send_kv, recv_kv, 0)
    own_kv[...] = acct[:, pl.ds(own_at, 64), :]

    phase(2 * partner, partner)
    turn(acct)
    send_q[...] = acct[...].astype(BF16)
    copy_q = exchange(send_q, recv_q, 1)

    cosine = cos_ref[...].reshape(8, 8, rows)
    sine = sin_ref[...].reshape(8, 8, rows)

    def rotate(field):
        a, b = field[:, :8, :], field[:, 8:, :]
        return jnp.concatenate([a * cosine - b * sine, b * cosine + a * sine], axis=1)

    def natural(field):
        return tn(field.reshape(128, rows).astype(BF16), perm).astype(BF16)

    copy_kv.wait()
    for head in range(2):
        k_at, v_at = 16 * head, 32 + 16 * head
        key = own_kv[:, k_at : k_at + 16, :] + recv_kv[:, k_at : k_at + 16, :].astype(F32)
        kv_ref[:rows, head * 256 : head * 256 + 128] = natural(rotate(key))
        value = own_kv[:, v_at : v_at + 16, :] + recv_kv[:, v_at : v_at + 16, :].astype(F32)
        kv_ref[:rows, head * 256 + 128 : head * 256 + 256] = natural(value)
    ids = jnp.broadcast_to(ids_ref[...].astype(F32), (ID_ROWS, rows)).astype(BF16)
    kv_ref[rows:, :] = jnp.concatenate([ids] * 4, axis=1)

    phase(2 * member, member)
    turn(acct)
    copy_q.wait()
    for head in range(8):
        at = pl.multiple_of(16 * lax.rem(head + 4 * member, 8), 16)
        up_t = nt(perm, qup_ref[:, head * 128 : (head + 1) * 128]).astype(BF16)
        adapter = jnp.dot(up_t, lr_t, preferred_element_type=F32).reshape(8, 16, rows)
        query = acct[:, pl.ds(at, 16), :] + recv_q[:, pl.ds(at, 16), :].astype(F32)
        query = query + ADAPTER_SCALE * adapter
        q_ref[:, head * 128 : (head + 1) * 128] = natural(rotate(query))


def attn_kernel(
    first_ref, q_ref, do_ref, kv_ref, ids_ref, xn_ref, lr_ref, qup_ref, cos_ref, sin_ref,
    out_ref, up_ref, ga_ref,
    qs, dos, row_max, row_sum, row_dot, out_acc, grad_acc, lin,
):
    me = lax.axis_index("ctx")
    rows = q_ref.shape[0]
    soft_scale = 1.0 / math.sqrt(HEAD_SIZE)
    group = QUERY_HEADS // KEY_VALUE_HEADS
    many = group * rows
    my_ids = ids_ref[...]

    for head in range(8):
        at = head * rows
        qs[at : at + rows, :] = q_ref[:, head * 128 : (head + 1) * 128]
        dos[at : at + rows, :] = do_ref[:, head * 128 : (head + 1) * 128]

    def part(head, kv_part, allowed, first):
        span = pl.ds(head * many, many)
        key = kv_part[:, head * 256 : head * 256 + 128]
        value = kv_part[:, head * 256 + 128 : head * 256 + 256]
        both = kv_part[:, head * 256 : head * 256 + 256]
        scores = nt(qs[span, :], key) * soft_scale
        scores = jnp.where(jnp.concatenate([allowed] * group, axis=0), scores, -1e30)
        top = jnp.max(scores, axis=-1, keepdims=True)
        if not first:
            top = jnp.maximum(top, row_max[span, :])
        expo = jnp.exp(scores - top)
        weighted = expo * nt(dos[span, :], value)
        total = jnp.sum(expo, axis=-1, keepdims=True)
        dot_total = jnp.sum(weighted, axis=-1, keepdims=True)
        new_out = jnp.dot(expo.astype(BF16), both, preferred_element_type=F32)
        new_grad = jnp.dot(weighted.astype(BF16), key, preferred_element_type=F32)
        if first:
            row_sum[span, :] = total
            row_dot[span, :] = dot_total
            out_acc[span, :] = new_out
            grad_acc[span, :] = new_grad
        else:
            decay = jnp.exp(row_max[span, :] - top)
            row_sum[span, :] = decay * row_sum[span, :] + total
            row_dot[span, :] = decay * row_dot[span, :] + dot_total
            out_acc[span, :] = decay * out_acc[span, :] + new_out
            grad_acc[span, :] = decay * grad_acc[span, :] + new_grad
        row_max[span, :] = top

    diag = kv_ref[me]
    key_ids = diag[rows : rows + 1, :128].astype(F32)
    qi = lax.broadcasted_iota(jnp.int32, (rows, rows), 0)
    ki = lax.broadcasted_iota(jnp.int32, (rows, rows), 1)
    allowed = (my_ids == key_ids) & (ki <= qi)
    for head in range(2):
        part(head, diag[:rows], allowed, True)

    lane = lax.broadcasted_iota(jnp.int32, (1, 2 * rows), 1)

    def step(t, carry):
        upper = me - 2 * t
        start = jnp.maximum(upper - 2, 0)
        pair = [kv_ref[start], kv_ref[start + 1]]
        both = jnp.concatenate([p[:rows] for p in pair], axis=0)
        key_ids = jnp.concatenate([p[rows : rows + 1, :128] for p in pair], axis=1).astype(F32)
        key_ids = jnp.where(lane < (upper - start) * rows, key_ids, -1.0)
        allowed = my_ids == key_ids
        for head in range(2):
            part(head, both, allowed, False)
        return carry

    lax.fori_loop(0, (me - first_ref[0] + 1) // 2, step, 0)

    cosine, sine = cos_ref[...], sin_ref[...]
    for head in range(8):
        at = head * rows
        span = slice(at, at + rows)
        inverse = 1.0 / row_sum[span, :]
        out_ref[:, head * 128 : (head + 1) * 128] = (out_acc[span, 128:] * inverse).astype(BF16)
        mean_dot = row_dot[span, :] * inverse
        grad = soft_scale * inverse * (grad_acc[span, :] - mean_dot * out_acc[span, :128])
        turned = pltpu.roll(grad * sine, 64, 1)
        lin[:, head * 128 : (head + 1) * 128] = (grad * cosine + turned).astype(BF16)
    up_ref[...] = ADAPTER_SCALE * jnp.dot(lr_ref[...], lin[...], preferred_element_type=F32)
    middle = (ADAPTER_SCALE * nt(qup_ref[...], lin[...])).astype(BF16)
    ga_ref[...] = jnp.dot(middle, xn_ref[...], preferred_element_type=F32)


def rope_tables(place, rows):
    positions = (place * rows + jnp.arange(rows, dtype=jnp.int32)).astype(F32)
    half = HEAD_SIZE // 2
    freqs = jnp.exp(jnp.arange(half, dtype=F32) * (-2.0 * math.log(ROPE_BASE) / HEAD_SIZE))
    angle = positions[:, None] * freqs[None, :]
    cosine, sine = jnp.cos(angle), jnp.sin(angle)
    def planes(table):
        return jnp.transpose(table.T.reshape(8, 8, rows), (1, 0, 2)).reshape(half, rows)

    wide_cos = jnp.concatenate([cosine, cosine], axis=-1)
    wide_sin = jnp.concatenate([-sine, sine], axis=-1)
    return planes(cosine), planes(sine), wide_cos, wide_sin


def on_device(
    layer_input, gain, codes, column_scale_quantized, block_second_scale,
    query_down_map, query_up_map, token_document, output_cotangent,
):
    rows, width = layer_input.shape
    place = lax.axis_index("ctx")
    cos_t, sin_t, cos_w, sin_w = rope_tables(place, rows)
    vm = pl.BlockSpec(memory_space=pltpu.VMEM)
    sm = pl.BlockSpec(memory_space=pltpu.SMEM)
    blocks = column_scale_quantized.shape[0]
    rank = query_up_map.shape[0]
    kv_width = 4 * HEAD_SIZE
    q, kv, xn, lr = pl.pallas_call(
        proj_kernel,
        out_shape=(
            jax.ShapeDtypeStruct((rows, query_up_map.shape[1]), BF16),
            jax.ShapeDtypeStruct((rows + ID_ROWS, kv_width), BF16),
            jax.ShapeDtypeStruct((rows, width), BF16),
            jax.ShapeDtypeStruct((rank, rows), BF16),
        ),
        in_specs=[vm] * 10,
        out_specs=(vm,) * 4,
        scratch_shapes=[
            pltpu.VMEM((24, blocks, 128), F32),
            pltpu.VMEM((8, blocks, 128), F32),
            pltpu.VMEM((rows, 1024), F32),
            pltpu.VMEM((8, 128, rows), F32),
            pltpu.VMEM((8, 64, rows), F32),
            pltpu.VMEM((8, 64, rows), BF16),
            pltpu.VMEM((8, 64, rows), BF16),
            pltpu.VMEM((8, 128, rows), BF16),
            pltpu.VMEM((8, 128, rows), BF16),
            pltpu.SemaphoreType.DMA((2,)),
            pltpu.SemaphoreType.DMA((2,)),
        ],
        compiler_params=pltpu.CompilerParams(
            collective_id=0, has_side_effects=True, vmem_limit_bytes=56 * 1024 * 1024
        ),
        name="project",
    )(
        layer_input, gain[None, :], codes, column_scale_quantized, block_second_scale[:, None],
        query_down_map.T, query_up_map, token_document[None, :], cos_t, sin_t,
    )
    all_kv = lax.all_gather(kv, "ctx", axis=0, tiled=False)
    all_ids = all_kv[:, rows, :rows].astype(F32)
    needed = (all_ids[:, -1] >= token_document[0].astype(F32)) & (
        jnp.arange(all_ids.shape[0]) <= place
    )
    first = jnp.argmax(needed).astype(jnp.int32)[None]
    heads_rows = 8 * rows
    attn, up, ga = pl.pallas_call(
        attn_kernel,
        out_shape=(
            jax.ShapeDtypeStruct(output_cotangent.shape, BF16),
            jax.ShapeDtypeStruct(query_up_map.shape, F32),
            jax.ShapeDtypeStruct((rank, width), F32),
        ),
        in_specs=[sm] + [vm] * 9,
        out_specs=(vm,) * 3,
        scratch_shapes=[
            pltpu.VMEM((heads_rows, 128), BF16),
            pltpu.VMEM((heads_rows, 128), BF16),
            pltpu.VMEM((heads_rows, 1), F32),
            pltpu.VMEM((heads_rows, 1), F32),
            pltpu.VMEM((heads_rows, 1), F32),
            pltpu.VMEM((heads_rows, 256), F32),
            pltpu.VMEM((heads_rows, 128), F32),
            pltpu.VMEM((rows, 1024), BF16),
        ],
        compiler_params=pltpu.CompilerParams(vmem_limit_bytes=56 * 1024 * 1024),
        name="attend",
    )(
        first, q, output_cotangent, all_kv, token_document.astype(F32)[:, None], xn, lr,
        query_up_map, cos_w, sin_w,
    )
    up = lax.psum(up, "ctx")
    ga = lax.psum(ga, ("ctx", "fsdp"))
    return attn, ga.T, up


def solution(mesh):
    return jax.shard_map(
        on_device,
        mesh=mesh,
        in_specs=(
            P("ctx", None),
            P(),
            P("fsdp", None),
            P("fsdp", None),
            P(),
            P(),
            P(None, "fsdp"),
            P("ctx"),
            P("ctx", "fsdp"),
        ),
        out_specs=(P("ctx", "fsdp"), P(), P(None, "fsdp")),
        check_vma=False,
    )
```

profile of v0, /device:TPU:0, one launch (start us, length us, event | category | flops | bytes accessed | tf_op | source)
XLA Modules:
  0.0 334.2 jit_solution(16420975947894687694)
XLA Ops:
  7.2 0.0 copy-start
  7.2 0.0 all-gather.3.cloned.1.call-start
  7.3 0.1 exp.16
  7.3 1.4 copy.14.bss_ref
  8.7 0.8 multiply_sine_fusion.1
  9.5 30.5 %project.1 = (bf16[128,1024]{1,0:T(8,128)(2,1)}, bf16[144,512]{1,0:T(8,128)(2,1)}, bf16[128,4096]{1,0:T(8,128)(2,1)}, bf16[16,128]{1,0:T(8,128)(2,1)}) custom-call(bf16[128,4096]{1,0:T(8,128)(2,1)} %x_ref.1, f32[1,4096]{1,0:T(1,128)} %bitcast.18, s32[2048,384]{1,0:T(8,128)} %codes_ref.1, s32[32,3072]{1,0:T(8,128)} %cs_ref.1, f32[64,1]{1,0:T(8,128)} %copy.14.bss_ref, ...), custom_call_target="tpu_custom_call" | custom-call | tf_op jit(solution)/shard_map/project/pallas_call | solution.py:317
  40.0 0.0 all-gather.3.cloned.1.call-update
  40.1 0.0 all-reduce.5.cloned.1.call-start
  40.1 0.0 copy-done
  40.2 0.7 copy.15.ids_ref
  40.9 0.3 fusion
  41.2 0.8 pad_maximum_fusion
  42.0 41.1 %all-gather.3.cloned.1.call-done = bf16[2304,512]{1,0:T(8,128)(2,1)} async-done(((bf16[144,512]{1,0:T(8,128)(2,1)}), bf16[2304,512]{1,0:T(8,128)(2,1)}) %all-gather.3.cloned.1.call-update) | async-done | bytes 2359312 | tf_op jit(solution)/shard_map/all_gather | solution.py:348
  83.0 0.8 slice.16
  83.8 0.2 fusion.1
  84.0 0.7 and_reduce_fusion
  84.7 5.5 %attend.1 = (bf16[128,1024]{1,0:T(8,128)(2,1)}, f32[16,1024]{1,0:T(8,128)}, f32[16,4096]{1,0:T(8,128)}) custom-call(s32[1]{0:T(128)} %bitcast.6.first_ref, bf16[128,1024]{1,0:T(8,128)(2,1)} %get-tuple-element.13.q_ref, bf16[128,1024]{1,0:T(8,128)(2,1)} %do_ref.1, bf16[16,144,512]{2,1,0:T(8,128)(2,1)} %bitcast.15, f32[128,1]{1,0:T(8,128)} %copy.15.ids_ref, ...), custom_call_target="tpu_custom_call" | custom-call | tf_op jit(solution)/shard_map/attend/pallas_call | solution.py:355
  90.3 0.0 all-reduce.5.cloned.1.call-update
  90.3 0.0 all-reduce.3.cloned.1.call-start
  90.3 0.7 all-reduce.3.cloned.1.call-update
  91.0 99.2 %all-reduce.5.cloned.1.call-done = f32[16,1024]{1,0:T(8,128)} async-done(((f32[16,1024]{1,0:T(8,128)}), f32[16,1024]{1,0:T(8,128)}) %all-reduce.5.cloned.1.call-update) | async-done | bytes 65552 | tf_op jit(solution)/shard_map/psum | solution.py:380
  190.2 134.2 %all-reduce.3.cloned.1.call-done = f32[4096,16]{0,1:T(8,128)} async-done(((f32[4096,16]{0,1:T(8,128)}), f32[4096,16]{0,1:T(8,128)}) %all-reduce.3.cloned.1.call-update) | async-done | bytes 262160 | tf_op jit(solution)/shard_map/psum | solution.py:381
  324.5 1.7 copy.21
  326.2 1.5 copy.22
  (5 shorter events, 0.0 us)
Async XLA Ops:
  7.2 32.9 %copy-start = (s32[128]{0:T(128)S(1)}, s32[128]{0:T(128)}, u32[]{:S(2)}) copy-start(s32[128]{0:T(128)} %param.16) | copy-start | bytes 1540
  7.2 75.9 %all-gather.3.cloned.1.call-start = ((), (), s32[]{:S(2)}) async-start(), calls=%async_computation.2 | async-start | bytes 2506752 | tf_op jit(solution)/shard_map/all_gather | solution.py:348
  40.1 150.2 %all-reduce.5.cloned.1.call-start = ((), (), s32[]{:S(2)}) async-start(), calls=%async_computation.1 | async-start | bytes 131072 | tf_op jit(solution)/shard_map/psum | solution.py:380
  90.3 234.2 %all-reduce.3.cloned.1.call-start = ((), (), s32[]{:S(2)}) async-start(), calls=%async_computation | async-start | bytes 524288 | tf_op jit(solution)/shard_map/psum | solution.py:381
Sparse Core Ops, SparseCore 0:
  40.2 42.8 all-gather.2
  90.4 99.7 all-reduce.4
  196.3 128.1 all-reduce.2
where the time goes:
time: 334 us
  waiting for transfers between devices  275 us (82%)
  Pallas kernels  36 us (11%)
  between operations  13.8 us (4%)
  local copies, waits for them, and re-layouts  6.1 us (2%)
    psum x1, waiting for transfers between devices, on_device(): ga = lax.psum(ga, ('ctx', 'fsdp'))  134 us
    psum x1, waiting for transfers between devices, on_device(): up = lax.psum(up, 'ctx')  99.2 us
    all_gather x1, waiting for transfers between devices, on_device(): all_kv = lax.all_gather(kv, 'ctx', axis=0, tiled=False)  41.1 us
    pallas_call x1, Pallas kernels, on_device(): pl.pallas_call(proj_kernel, out_shape=(jax.ShapeDtypeStruct((rows, query_...  30.5 us
  transfers between devices with their start and end apart: 3, of which 3 were waited for; matrix products, arithmetic and copies ran while one was open for 1% of the time, Pallas kernels for 0%

commit v1 on v0

--- a/solution.py
+++ b/solution.py
@@ -288,6 +288,128 @@
     ga_ref[...] = jnp.dot(middle, xn_ref[...], preferred_element_type=F32)
 
 
+def reduce_kernel(
+    counts, ga_ref, up_ref, ga_out, up_out,
+    ga_part, ga_in, ga_sum, ga_all, up_part, up_in, up_sum, up_all, sems,
+):
+    ctx_count, fsdp_count = counts
+    total = ctx_count * fsdp_count
+    ctx, fsdp = lax.axis_index("ctx"), lax.axis_index("fsdp")
+    me = ctx * fsdp_count + fsdp
+    ga_owners, up_owners = ga_part.shape[0], up_part.shape[0]
+    ga_stride, up_stride = total // ga_owners, ctx_count // up_owners
+    tiles = up_owners // 2
+
+    barrier = pltpu.get_barrier_semaphore()
+
+    def greet(step, carry):
+        other = lax.rem(me + step, total)
+        pl.semaphore_signal(
+            barrier, inc=1, device_id=(other // fsdp_count, lax.rem(other, fsdp_count)),
+            device_id_type=MESH,
+        )
+        return carry
+
+    lax.fori_loop(1, total, greet, 0)
+
+    for j in range(ga_owners):
+        ga_part[j] = ga_ref[:, j * 128 : (j + 1) * 128].astype(BF16)
+    for j in range(up_owners):
+        row, col = 8 * (j // tiles), 128 * (j % tiles)
+        up_part[j] = up_ref[row : row + 8, col : col + 128]
+    pl.semaphore_wait(barrier, total - 1)
+
+    def send(src, dst, number, ctx_to, fsdp_to):
+        pltpu.make_async_remote_copy(
+            src_ref=src, dst_ref=dst, send_sem=sems.at[2 * number],
+            recv_sem=sems.at[2 * number + 1], device_id=(ctx_to, fsdp_to),
+            device_id_type=MESH,
+        ).start()
+
+    def keep(src, dst, number):
+        pltpu.make_async_copy(src, dst, sems.at[2 * number + 1]).start()
+
+    def await_all(buffer, number, slot):
+        pltpu.make_async_copy(buffer, buffer, sems.at[2 * number + slot]).wait()
+
+    up_mine, ga_mine = ctx // up_stride, me // ga_stride
+    up_owner, ga_owner = lax.rem(ctx, up_stride) == 0, lax.rem(me, ga_stride) == 0
+
+    def scatter_up(step, carry):
+        j = lax.rem(up_mine + step, up_owners)
+        to = j * up_stride
+
+        @pl.when(to != ctx)
+        def _():
+            send(up_part.at[j], up_in.at[ctx], 0, to, fsdp)
+
+        return carry
+
+    def scatter_ga(step, carry):
+        j = lax.rem(ga_mine + step, ga_owners)
+        to = j * ga_stride
+
+        @pl.when(to != me)
+        def _():
+            send(
+                ga_part.at[j], ga_in.at[me], 1, to // fsdp_count, lax.rem(to, fsdp_count)
+            )
+
+        return carry
+
+    lax.fori_loop(0, up_owners, scatter_up, 0)
+    lax.fori_loop(0, ga_owners, scatter_ga, 0)
+
+    @pl.when(up_owner)
+    def _():
+        keep(up_part.at[up_mine], up_in.at[ctx], 0)
+        await_all(up_in, 0, 1)
+        up_sum[...] = jnp.sum(up_in[...], axis=0)
+
+        def spread(step, carry):
+            send(up_sum, up_all.at[up_mine], 2, lax.rem(ctx + step, ctx_count), fsdp)
+            return carry
+
+        lax.fori_loop(1, ctx_count, spread, 0)
+        keep(up_sum, up_all.at[up_mine], 2)
+
+    @pl.when(ga_owner)
+    def _():
+        keep(ga_part.at[ga_mine], ga_in.at[me], 1)
+        await_all(ga_in, 1, 1)
+        ga_sum[...] = jnp.sum(ga_in[...].astype(F32), axis=0).astype(BF16)
+
+        def spread(step, carry):
+            to = lax.rem(me + step, total)
+            send(ga_sum, ga_all.at[ga_mine], 3, to // fsdp_count, lax.rem(to, fsdp_count))
+            return carry
+
+        lax.fori_loop(1, total, spread, 0)
+        keep(ga_sum, ga_all.at[ga_mine], 3)
+
+    await_all(up_all, 2, 1)
+    for j in range(up_owners):
+        row, col = 8 * (j // tiles), 128 * (j % tiles)
+        up_out[row : row + 8, col : col + 128] = up_all[j]
+    await_all(ga_all, 3, 1)
+    for j in range(ga_owners):
+        ga_out[:, j * 128 : (j + 1) * 128] = ga_all[j].astype(F32)
+
+    def drain(buffer, number, sent):
+        @pl.when(sent > 0)
+        def _():
+            def one(step, carry):
+                pltpu.make_async_copy(buffer, buffer, sems.at[2 * number]).wait()
+                return carry
+
+            lax.fori_loop(0, sent, one, 0)
+
+    drain(up_part.at[0], 0, up_owners - up_owner.astype(jnp.int32))
+    drain(ga_part.at[0], 1, ga_owners - ga_owner.astype(jnp.int32))
+    drain(up_sum, 2, jnp.where(up_owner, ctx_count - 1, 0))
+    drain(ga_sum, 3, jnp.where(ga_owner, total - 1, 0))
+
+
 def rope_tables(place, rows):
     positions = (place * rows + jnp.arange(rows, dtype=jnp.int32)).astype(F32)
     half = HEAD_SIZE // 2
@@ -303,7 +425,7 @@
 
 
 def on_device(
-    layer_input, gain, codes, column_scale_quantized, block_second_scale,
+    counts, layer_input, gain, codes, column_scale_quantized, block_second_scale,
     query_down_map, query_up_map, token_document, output_cotangent,
 ):
     rows, width = layer_input.shape
@@ -377,14 +499,39 @@
         first, q, output_cotangent, all_kv, token_document.astype(F32)[:, None], xn, lr,
         query_up_map, cos_w, sin_w,
     )
-    up = lax.psum(up, "ctx")
-    ga = lax.psum(ga, ("ctx", "fsdp"))
+    total = counts[0] * counts[1]
+    ga_owners = math.gcd(total, width // 128)
+    up_owners = math.gcd(counts[0], 2 * (up.shape[1] // 128))
+    ga, up = pl.pallas_call(
+        functools.partial(reduce_kernel, counts),
+        out_shape=(
+            jax.ShapeDtypeStruct((rank, width), F32),
+            jax.ShapeDtypeStruct(query_up_map.shape, F32),
+        ),
+        in_specs=[vm] * 2,
+        out_specs=(vm,) * 2,
+        scratch_shapes=[
+            pltpu.VMEM((ga_owners, rank, 128), BF16),
+            pltpu.VMEM((total, rank, 128), BF16),
+            pltpu.VMEM((rank, 128), BF16),
+            pltpu.VMEM((ga_owners, rank, 128), BF16),
+            pltpu.VMEM((up_owners, 8, 128), F32),
+            pltpu.VMEM((counts[0], 8, 128), F32),
+            pltpu.VMEM((8, 128), F32),
+            pltpu.VMEM((up_owners, 8, 128), F32),
+            pltpu.SemaphoreType.DMA((8,)),
+        ],
+        compiler_params=pltpu.CompilerParams(
+            collective_id=1, has_side_effects=True, vmem_limit_bytes=56 * 1024 * 1024
+        ),
+        name="reduce",
+    )(ga, up)
     return attn, ga.T, up
 
 
 def solution(mesh):
     return jax.shard_map(
-        on_device,
+        functools.partial(on_device, (mesh.shape["ctx"], mesh.shape["fsdp"])),
         mesh=mesh,
         in_specs=(
             P("ctx", None),

time: 334 us -> 133 us (0.40)
  waiting for transfers between devices: 275 us -> 41.1 us
  Pallas kernels: 36 us -> 68 us
    psum x2 -> x0, waiting for transfers between devices: 233 us -> none  [the longest x1 134 us: on_device(): ga = lax.psum(ga, ('ctx', 'fsdp'))]
    pallas_call x0 -> x1, Pallas kernels: none -> 31.9 us  [on_device(): pl.pallas_call(functools.partial(reduce_kernel, counts), out_shape=(jax.S...]
  transfers between devices with their start and end apart: 3 -> 1, of which waited for: 3 -> 1; matrix products, arithmetic and copies ran while one was open for 1% -> 1% of each run, Pallas kernels for 0% -> 0%
where the time goes in v1:
time: 133 us; the launch traced here: 132 us
  Pallas kernels  68 us (51%)
  waiting for transfers between devices  41.1 us (31%)
  between operations  14.1 us (11%)
  local copies, waits for them, and re-layouts  6.1 us (5%)
  other arithmetic  2.83 us (2%)
    all_gather x1, waiting for transfers between devices, on_device(): all_kv = lax.all_gather(kv, 'ctx', axis=0, tiled=False)  41.1 us
    pallas_call x1, Pallas kernels, on_device(): pl.pallas_call(functools.partial(reduce_kernel, counts), out_shape=(jax.S...  31.9 us
    pallas_call x1, Pallas kernels, on_device(): pl.pallas_call(proj_kernel, out_shape=(jax.ShapeDtypeStruct((rows, query_...  30.5 us
    pallas_call x1, Pallas kernels, on_device(): pl.pallas_call(attn_kernel, out_shape=(jax.ShapeDtypeStruct(output_cotang...  5.54 us
    unnamed x5, local copies, waits for them, and re-layouts  3.16 us
  transfers between devices with their start and end apart: 1, of which 1 were waited for; matrix products, arithmetic and copies ran while one was open for 1% of the time, Pallas kernels for 0%

profile of v1, /device:TPU:0, one launch (start us, length us, event | category | flops | bytes accessed | tf_op | source)
XLA Modules:
  0.0 132.2 jit_solution(4803484027142104663)
XLA Ops:
  7.2 0.0 copy-start
  7.2 0.0 all-gather.3.cloned.1.call-start
  7.3 0.1 exp.16
  7.3 1.4 %copy.14.bss_ref = f32[64,1]{1,0:T(8,128)} copy(f32[64,1]{0,1:T(1,128)} %bitcast.20) | data formatting | bytes 512 | tf_op jit(solution)/shard_map/broadcast_in_dim | solution.py:467
  8.7 0.8 multiply_sine_fusion.1
  9.5 30.5 %project.1 = (bf16[128,1024]{1,0:T(8,128)(2,1)}, bf16[144,512]{1,0:T(8,128)(2,1)}, bf16[128,4096]{1,0:T(8,128)(2,1)}, bf16[16,128]{1,0:T(8,128)(2,1)}) custom-call(bf16[128,4096]{1,0:T(8,128)(2,1)} %x_ref.1, f32[1,4096]{1,0:T(1,128)} %bitcast.18, s32[2048,384]{1,0:T(8,128)} %codes_ref.1, s32[32,3072]{1,0:T(8,128)} %cs_ref.1, f32[64,1]{1,0:T(8,128)} %copy.14.bss_ref, ...), custom_call_target="tpu_custom_call" | custom-call | tf_op jit(solution)/shard_map/project/pallas_call | solution.py:439
  40.0 0.0 all-gather.3.cloned.1.call-update
  40.1 0.0 copy-done
  40.1 0.7 copy.15.ids_ref
  40.9 0.3 fusion
  41.2 0.8 pad_maximum_fusion
  41.9 41.1 %all-gather.3.cloned.1.call-done = bf16[2304,512]{1,0:T(8,128)(2,1)} async-done(((bf16[144,512]{1,0:T(8,128)(2,1)}), bf16[2304,512]{1,0:T(8,128)(2,1)}) %all-gather.3.cloned.1.call-update) | async-done | bytes 2359312 | tf_op jit(solution)/shard_map/all_gather | solution.py:470
  83.0 0.8 slice.16
  83.8 0.2 fusion.1
  84.0 0.7 and_reduce_fusion
  84.7 5.5 %attend.1 = (bf16[128,1024]{1,0:T(8,128)(2,1)}, f32[16,1024]{1,0:T(8,128)}, f32[16,4096]{1,0:T(8,128)}) custom-call(s32[1]{0:T(128)} %bitcast.6.first_ref, bf16[128,1024]{1,0:T(8,128)(2,1)} %get-tuple-element.15.q_ref, bf16[128,1024]{1,0:T(8,128)(2,1)} %do_ref.1, bf16[16,144,512]{2,1,0:T(8,128)(2,1)} %bitcast.15, f32[128,1]{1,0:T(8,128)} %copy.15.ids_ref, ...), custom_call_target="tpu_custom_call" | custom-call | tf_op jit(solution)/shard_map/attend/pallas_call | solution.py:477
  90.3 31.9 %reduce.22 = (f32[16,4096]{1,0:T(8,128)}, f32[16,1024]{1,0:T(8,128)}) custom-call(f32[16,4096]{1,0:T(8,128)} %get-tuple-element.19.ga_ref, f32[16,1024]{1,0:T(8,128)} %get-tuple-element.20.up_ref), custom_call_target="tpu_custom_call" | custom-call | tf_op jit(solution)/shard_map/reduce/pallas_call | solution.py:505
  122.2 1.7 %copy.21 = f32[4096,16]{0,1:T(8,128)} copy(f32[4096,16]{0,1:T(8,128)} %bitcast.16) | data formatting | bytes 524288
  123.9 1.5 %copy.22 = f32[16,1024]{1,0:T(8,128)} copy(f32[16,1024]{1,0:T(8,128)} %get-tuple-element.35) | data formatting | bytes 131072
  (5 shorter events, 0.0 us)
Async XLA Ops:
  7.2 32.9 %copy-start = (s32[128]{0:T(128)S(1)}, s32[128]{0:T(128)}, u32[]{:S(2)}) copy-start(s32[128]{0:T(128)} %param.16) | copy-start | bytes 1540
  7.2 75.9 %all-gather.3.cloned.1.call-start = ((), (), s32[]{:S(2)}) async-start(), calls=%async_computation | async-start | bytes 2506752 | tf_op jit(solution)/shard_map/all_gather | solution.py:470
Sparse Core Ops, SparseCore 0:
  40.2 42.8 all-gather.2

commit v2 on v0

v2 whole, which is shorter than its diff:
```python
import math
import functools

import jax
import jax.numpy as jnp
from jax import lax
from jax.experimental import pallas as pl
from jax.experimental.pallas import tpu as pltpu
from jax.sharding import PartitionSpec as P

HEAD_SIZE = 128
ADAPTER_SCALE = 2.0
ROPE_BASE = 500000.0
MESH = pl.DeviceIdType.MESH
F32 = jnp.float32
BF16 = jnp.bfloat16
I16 = jnp.int16

NF4_LEVELS = [
    -1.0,
    -0.6961928009986877,
    -0.5250730514526367,
    -0.39491748809814453,
    -0.28444138169288635,
    -0.18477343022823334,
    -0.09105003625154495,
    0.0,
    0.07958029955625534,
    0.16093020141124725,
    0.24611230194568634,
    0.33791524171829224,
    0.44070982933044434,
    0.5626170039176941,
    0.7229568362236023,
    1.0,
]


def take_lanes(values, index):
    return jnp.take_along_axis(values, index, axis=1, mode="promise_in_bounds")


def dot(a, b):
    return jnp.dot(a, b, preferred_element_type=F32)


def nt(a, b):
    return lax.dot_general(a, b, (((1,), (1,)), ((), ())), preferred_element_type=F32)


def tn(a, b):
    return lax.dot_general(a, b, (((0,), (0,)), ((), ())), preferred_element_type=F32)


def eye(size):
    row = lax.broadcasted_iota(jnp.int32, (size, size), 0)
    col = lax.broadcasted_iota(jnp.int32, (size, size), 1)
    return (row == col).astype(F32).astype(BF16)


def step_kernel(
    counts,
    x_ref, gain_ref, codes_ref, cs_ref, bss_ref, qdown_ref, qup_ref, ids_ref, cos_ref, sin_ref,
    do_ref,
    out_ref, ga_out, up_out,
    scl, vscl, acc, acct, xn, own_kv, send_kv, recv_kv, own_q, send_q, recv_q,
    do_all, ids_all, kv_all, queries, cotans, vk, row_max, out_acc, grad_acc, lin,
    out_stage, out_in,
    ga_part, ga_in, ga_sum, ga_all, up_part, up_in, up_sum, up_all,
    pair_send, pair_recv, block_send, block_recv, sems,
):
    ctx_count, fsdp_count = counts
    total = ctx_count * fsdp_count
    ctx, member = lax.axis_index("ctx"), lax.axis_index("fsdp")
    me = ctx * fsdp_count + member
    partner = 1 - member
    chip, core = ctx // 2, lax.rem(ctx, 2)
    outer, inner = chip // 2, lax.rem(chip, 2)
    sibling = ctx + 1 - 2 * core
    chips = ctx_count // 2
    rows, width = x_ref.shape
    tokens = 2 * rows
    depth = codes_ref.shape[0]
    half_depth = depth // 2
    blocks = cs_ref.shape[0]
    block_rows = depth // blocks
    half_blocks = blocks // 2

    barrier = pltpu.get_barrier_semaphore()

    def greet(step, carry):
        other = lax.rem(me + step, total)
        pl.semaphore_signal(
            barrier, inc=1, device_id=(other // fsdp_count, lax.rem(other, fsdp_count)),
            device_id_type=MESH,
        )
        return carry

    lax.fori_loop(1, total, greet, 0)

    mine_at = pl.multiple_of(core * rows, rows)
    other_at = pl.multiple_of((1 - core) * rows, rows)
    for r in range(0, rows, 16):
        wide = x_ref[r : r + 16, :].astype(F32)
        inverse = lax.rsqrt(jnp.mean(wide * wide, axis=-1, keepdims=True) + 1e-05)
        xn[pl.ds(pl.multiple_of(mine_at + r, 16), 16), :] = (
            wide * inverse * gain_ref[...]
        ).astype(BF16)
    ids_all[:, pl.ds(mine_at, rows)] = jnp.broadcast_to(
        ids_ref[...].astype(F32), (16, rows)
    ).astype(BF16)
    half_columns = do_ref.shape[1] // 2
    mine_columns = pl.multiple_of(core * half_columns, 128)
    other_columns = pl.multiple_of((1 - core) * half_columns, 128)
    do_all[pl.ds(mine_at, rows), :] = do_ref[:, pl.ds(mine_columns, half_columns)]

    pl.semaphore_wait(barrier, total - 1)

    def pair_copy(src, dst, number, device):
        copy = pltpu.make_async_remote_copy(
            src_ref=src, dst_ref=dst, send_sem=pair_send.at[number],
            recv_sem=pair_recv.at[number], device_id=device, device_id_type=MESH,
        )
        copy.start()
        return copy

    across = (sibling, member)
    beside = (ctx, partner)
    span = pl.ds(mine_at, rows)
    copy_x = pair_copy(xn.at[span], xn.at[span], 0, across)
    copy_ids = pair_copy(ids_all.at[:, span], ids_all.at[:, span], 1, across)
    copy_do = pair_copy(
        do_ref.at[:, pl.ds(other_columns, half_columns)], do_all.at[span], 2, across
    )

    lane = lax.broadcasted_iota(jnp.int32, (blocks, 128), 1)
    second = bss_ref[pl.ds(pl.multiple_of(member * blocks, 8), blocks), :]
    for tile in range(3):
        source = [
            (cs_ref[:, tile * 1024 + m * 128 : tile * 1024 + (m + 1) * 128].astype(F32) + 1.0)
            / 256.0
            * second
            for m in range(8)
        ]
        for n in range(8):
            index = 8 * (lane % 16) + n
            picked = take_lanes(source[0], index)
            for m in range(1, 8):
                picked = jnp.where(lane // 16 == m, take_lanes(source[m], index), picked)
            scl[tile * 8 + n] = picked

    pr = lax.broadcasted_iota(jnp.int32, (128, 128), 0)
    pd = lax.broadcasted_iota(jnp.int32, (128, 128), 1)
    perm = (pd == 8 * (pr % 16) + pr // 16).astype(F32).astype(BF16)
    eye_wide = eye(256)

    chunk = 512
    per_chunk = chunk // block_rows
    short_lane = lax.broadcasted_iota(jnp.int32, (block_rows, 128), 1)
    half_lane = lax.broadcasted_iota(jnp.int32, (half_blocks, 128), 1)
    long_lane = lax.broadcasted_iota(jnp.int32, (tokens, 128), 1)
    levels = [jnp.full((block_rows, 128), level, BF16) for level in NF4_LEVELS]

    def phase(paired, tile, half):
        if paired:
            shift = 16 + 96 * core

            def chosen(lanes):
                return lax.rem(lanes // 16, 2) == core

            def words_at(at):
                return jnp.where(
                    short_lane < 64,
                    codes_ref[pl.ds(at, block_rows), 128:256],
                    codes_ref[pl.ds(at, block_rows), 256:384],
                )
        else:
            shift = 64
            tile_at = pl.multiple_of(tile * 128, 128)

            def chosen(lanes):
                return lanes // 64 == half

            def words_at(at):
                return codes_ref[pl.ds(at, block_rows), pl.ds(tile_at, 128)]

        for n in range(8):
            if paired:
                scale = jnp.where(lane < 64, scl[8 + n], scl[16 + n])
            else:
                scale = scl[tile * 8 + n]
            vscl[n] = jnp.where(
                chosen(half_lane), scale[:half_blocks], pltpu.roll(scale[half_blocks:], shift, 1)
            )
        acc[...] = jnp.zeros_like(acc)
        first = chosen(short_lane)

        def step(k, carry):
            at = pl.multiple_of(member * depth + k * chunk, 128)
            lower = xn[:, pl.ds(at, chunk)]
            upper = xn[:, pl.ds(pl.multiple_of(at + half_depth, 128), chunk)]
            low_words, high_words = [], []
            for b in range(per_chunk):
                row = pl.multiple_of(k * chunk + b * block_rows, block_rows)
                words = jnp.where(
                    first,
                    words_at(row),
                    pltpu.roll(words_at(pl.multiple_of(row + half_depth, block_rows)), shift, 1),
                )
                low_words.append(words.astype(I16))
                high_words.append(jnp.right_shift(words, 16).astype(I16))
            for pair in range(4):
                planes = []
                for n in (2 * pair, 2 * pair + 1):
                    pieces = []
                    for b in range(per_chunk):
                        words = low_words[b] if n < 4 else high_words[b]
                        values = levels
                        for bit in range(4):
                            place = 4 * (n % 4) + bit
                            mark = 1 << place if place < 15 else -(1 << 15)
                            mask = (words & jnp.int16(mark)) != 0
                            values = [
                                jnp.where(mask, values[v + 1], values[v])
                                for v in range(0, len(values), 2)
                            ]
                        scale = vscl[n, pl.ds(k * per_chunk + b, 1), :]
                        pieces.append(values[0] * scale.astype(BF16))
                    planes.append(jnp.concatenate(pieces, axis=0))
                weight = jnp.concatenate(planes, axis=1)
                columns = slice(pair * 256, (pair + 1) * 256)
                acc[0, :, columns] += dot(lower, weight)
                acc[1, :, columns] += dot(upper, weight)
            return carry

        lax.fori_loop(0, half_depth // chunk, step, 0)
        keep = chosen(long_lane)
        for n in range(8):
            columns = slice(n * 128, (n + 1) * 128)
            acct[n] = jnp.where(keep, acc[0, :, columns], acc[1, :, columns]).T

    copy_x.wait()
    copy_ids.wait()
    copy_do.wait()

    def kv_field(group, part):
        at = pl.multiple_of(64 * group, 64) + 32 * part
        return acct[:, pl.ds(pl.multiple_of(at, 32), 16), :] + acct[
            :, pl.ds(pl.multiple_of(at + 16, 16), 16), :
        ]

    phase(True, 0, 0)
    for part in range(2):
        send_kv[:, 16 * part : 16 * part + 16, :] = kv_field(partner, part).astype(BF16)
    copy_kv = pair_copy(send_kv, recv_kv, 3, beside)
    for part in range(2):
        own_kv[:, 16 * part : 16 * part + 16, :] = kv_field(member, part)

    place = 3 * partner + core
    phase(False, place // 2, lax.rem(place, 2))
    send_q[...] = (acct[:, :64, :] + acct[:, 64:, :]).astype(BF16)
    copy_q = pair_copy(send_q, recv_q, 4, beside)

    place = 3 * member + core
    phase(False, place // 2, lax.rem(place, 2))
    own_q[...] = acct[:, :64, :] + acct[:, 64:, :]

    cosine = cos_ref[...].reshape(8, 8, tokens)
    sine = sin_ref[...].reshape(8, 8, tokens)

    def rotate(field):
        a, b = field[:, :8, :], field[:, 8:, :]
        return jnp.concatenate([a * cosine - b * sine, b * cosine + a * sine], axis=1)

    copy_kv.wait()
    key = own_kv[:, :16, :] + recv_kv[:, :16, :].astype(F32)
    value = own_kv[:, 16:, :] + recv_kv[:, 16:, :].astype(F32)
    fields = jnp.concatenate(
        [value.reshape(128, tokens).astype(BF16), rotate(key).reshape(128, tokens).astype(BF16)],
        axis=0,
    )
    kv_all[chip, :tokens, :] = tn(fields, eye_wide).astype(BF16)
    kv_all[chip, tokens:, :] = ids_all[...]

    def send_block(block, to_chip):
        pltpu.make_async_remote_copy(
            src_ref=kv_all.at[block], dst_ref=kv_all.at[block],
            send_sem=block_send.at[0], recv_sem=block_recv.at[block],
            device_id=(2 * to_chip + core, member), device_id_type=MESH,
        ).start()

    def await_block(block):
        pltpu.make_async_copy(kv_all.at[block], kv_all.at[block], block_recv.at[block]).wait()

    @pl.when(inner == 0)
    def _():
        send_block(chip, chip + 1)

    def along(step, carry):
        send_block(chip, chip + 2 * step)
        return carry

    lax.fori_loop(1, chips // 2 - outer, along, 0)

    lr_t = nt(qdown_ref[...], xn[...]).astype(BF16)
    my_ids = ids_all[...]
    heads = own_q.shape[1] // 16
    local = pl.multiple_of(core * heads * 128, 128)
    marks = lax.broadcasted_iota(jnp.int32, (128, tokens), 0).astype(F32)
    tags = (marks == jnp.broadcast_to(my_ids[:1].astype(F32), (128, tokens))).astype(F32)
    tags = tags.astype(BF16)
    for head in range(heads):
        columns = slice(head * tokens, (head + 1) * tokens)
        queries[128:, columns] = tags
        cotans[:, columns] = nt(perm, do_all[:, head * 128 : (head + 1) * 128]).astype(BF16)

    copy_q.wait()
    for head in range(heads):
        columns = slice(head * tokens, (head + 1) * tokens)
        up_cols = qup_ref[:, pl.ds(pl.multiple_of(local + head * 128, 128), 128)]
        adapter = dot(nt(perm, up_cols).astype(BF16), lr_t).reshape(8, 16, tokens)
        query = own_q[:, 16 * head : 16 * head + 16, :]
        query = query + recv_q[:, 16 * head : 16 * head + 16, :].astype(F32)
        query = query + ADAPTER_SCALE * adapter
        queries[:128, columns] = rotate(query).reshape(128, tokens).astype(BF16)

    soft_scale = 1.0 / math.sqrt(HEAD_SIZE)
    log_scale = soft_scale / math.log(2.0)
    tag_row = lax.broadcasted_iota(jnp.int32, (16, tokens), 0).astype(F32)
    spread_row = lax.broadcasted_iota(jnp.int32, (16, 128), 0)
    spread_lane = lax.broadcasted_iota(jnp.int32, (16, 128), 1)
    spread_tags = (spread_row == spread_lane).astype(F32).astype(BF16)
    vk[256:, :] = jnp.ones((16, tokens), BF16)

    def attend(block, diagonal):
        both = kv_all[block, :tokens, :]
        block_ids = kv_all[block, tokens:, :].astype(F32)
        barred = jnp.where(block_ids == tag_row, 0.0, -1e30).astype(BF16)
        barred = tn(barred, spread_tags).astype(BF16)
        lhs = jnp.concatenate([both[:, 128:], barred], axis=1)
        vk[:256, :] = nt(eye_wide, both).astype(BF16)
        for head in range(heads):
            columns = slice(head * tokens, (head + 1) * tokens)
            row = slice(8 * head, 8 * head + 1)
            scores = dot(lhs, queries[:, columns]) * log_scale
            if diagonal:
                ki = lax.broadcasted_iota(jnp.int32, (tokens, tokens), 0)
                qi = lax.broadcasted_iota(jnp.int32, (tokens, tokens), 1)
                scores = jnp.where(ki <= qi, scores, -1e30)
            top = jnp.max(scores, axis=0, keepdims=True)
            if not diagonal:
                before = row_max[row, :]
                top = jnp.maximum(top, before)
            expo = jnp.exp2(scores - top)
            weighted = expo * dot(both[:, :128], cotans[:, columns])
            new_out = dot(vk[...], expo.astype(BF16))
            new_grad = dot(vk[128:, :], weighted.astype(BF16))
            row_max[row, :] = top
            if diagonal:
                out_acc[head] = new_out
                grad_acc[head] = new_grad
            else:
                decay = jnp.exp2(before - top)
                out_acc[head] = decay * out_acc[head] + new_out
                grad_acc[head] = decay * grad_acc[head] + new_grad

    attend(chip, True)

    def visit(step, carry):
        place = step - inner
        odd = lax.rem(place + 2, 2) == 1
        ahead = (place + 1) // 2

        @pl.when(((step == 0) | odd) & (ahead < outer))
        def _():
            block = 2 * (outer - 1 - ahead) + inner
            await_block(block)
            send_block(block, 2 * outer + 1 - inner)

        crossed = 2 * (outer - 1 - (place - 1) // 2) + 1 - inner
        crossed = jnp.where(place < 0, chip - 1, crossed)
        column = 2 * (outer - 1 - place // 2) + inner
        block = jnp.where(odd, crossed, column)

        @pl.when(odd)
        def _():
            await_block(block)

        attend(block, False)
        return carry

    lax.fori_loop(0, chip, visit, 0)

    middle = jnp.zeros((16, tokens), F32)
    back = 16 * (pd % 8) + pd // 8
    for head in range(heads):
        inverse = 1.0 / out_acc[head, 256:257, :]
        out = (out_acc[head, :128, :] * inverse).astype(BF16)
        out_stage[:, head * 128 : (head + 1) * 128] = tn(out, perm).astype(BF16)
    mine_out = pl.ds(mine_at, rows)
    copy_out = pair_copy(out_stage.at[pl.ds(other_at, rows)], out_in, 5, across)
    out_ref[:, pl.ds(mine_columns, half_columns)] = out_stage[mine_out, :]
    up_owners = up_part.shape[0]
    half_up = up_owners // 2
    for head in range(heads):
        inverse = 1.0 / out_acc[head, 256:257, :]
        mean_dot = grad_acc[head, 128:129, :] * inverse
        grad = grad_acc[head, :128, :] - mean_dot * out_acc[head, 128:256, :]
        grad = (soft_scale * inverse * grad).reshape(8, 16, tokens)
        a, b = grad[:, :8, :], grad[:, 8:, :]
        turned = jnp.concatenate([a * cosine + b * sine, b * cosine - a * sine], axis=1)
        lin_t = turned.reshape(128, tokens).astype(BF16)
        up_cols = qup_ref[:, pl.ds(pl.multiple_of(local + head * 128, 128), 128)]
        middle = middle + dot(nt(up_cols, perm).astype(BF16), lin_t)
        up = take_lanes(ADAPTER_SCALE * nt(lr_t, lin_t), back[:16])
        up_part[2 * head] = up[:8]
        up_part[2 * head + 1] = up[8:]
    middle = (ADAPTER_SCALE * middle).astype(BF16)
    ga_owners = ga_part.shape[0]
    for j in range(ga_owners):
        ga_part[j] = dot(middle, xn[:, j * 128 : (j + 1) * 128]).astype(BF16)

    up_pieces = up_part.shape[0]
    up_stride, ga_stride = chips // up_pieces, total // ga_owners
    up_mine, ga_mine = chip // up_stride, me // ga_stride
    up_owner, ga_owner = lax.rem(chip, up_stride) == 0, lax.rem(me, ga_stride) == 0
    up_slot = core * up_pieces + up_mine

    def send(src, dst, number, ctx_to, fsdp_to):
        pltpu.make_async_remote_copy(
            src_ref=src, dst_ref=dst, send_sem=sems.at[2 * number],
            recv_sem=sems.at[2 * number + 1], device_id=(ctx_to, fsdp_to),
            device_id_type=MESH,
        ).start()

    def hold(src, dst, number):
        pltpu.make_async_copy(src, dst, sems.at[2 * number + 1]).start()

    def await_all(buffer, number):
        pltpu.make_async_copy(buffer, buffer, sems.at[2 * number + 1]).wait()

    def scatter_up(step, carry):
        j = lax.rem(up_mine + step, up_pieces)
        to = j * up_stride

        @pl.when(to != chip)
        def _():
            send(up_part.at[j], up_in.at[chip], 0, 2 * to + core, member)

        return carry

    def scatter_ga(step, carry):
        j = lax.rem(ga_mine + step, ga_owners)
        to = j * ga_stride

        @pl.when(to != me)
        def _():
            send(ga_part.at[j], ga_in.at[me], 1, to // fsdp_count, lax.rem(to, fsdp_count))

        return carry

    lax.fori_loop(0, ga_owners, scatter_ga, 0)
    lax.fori_loop(0, up_pieces, scatter_up, 0)

    copy_out.wait()
    out_ref[:, pl.ds(other_columns, half_columns)] = out_in[...]

    @pl.when(ga_owner)
    def _():
        hold(ga_part.at[ga_mine], ga_in.at[me], 1)
        await_all(ga_in, 1)
        ga_sum[...] = jnp.sum(ga_in[...].astype(F32), axis=0).astype(BF16)

        def spread(step, carry):
            to = lax.rem(me + step, total)
            send(ga_sum, ga_all.at[ga_mine], 3, to // fsdp_count, lax.rem(to, fsdp_count))
            return carry

        lax.fori_loop(1, total, spread, 0)
        hold(ga_sum, ga_all.at[ga_mine], 3)

    @pl.when(up_owner)
    def _():
        hold(up_part.at[up_mine], up_in.at[chip], 0)
        await_all(up_in, 0)
        up_sum[...] = jnp.sum(up_in[...], axis=0)

        def spread(step, carry):
            send(up_sum, up_all.at[up_slot], 2, lax.rem(ctx + step, ctx_count), member)
            return carry

        lax.fori_loop(1, ctx_count, spread, 0)
        hold(up_sum, up_all.at[up_slot], 2)

    await_all(ga_all, 3)
    for j in range(ga_owners):
        ga_out[:, j * 128 : (j + 1) * 128] = ga_all[j].astype(F32)
    await_all(up_all, 2)
    for j in range(2 * up_pieces):
        for part in range(up_all.shape[1] // 8):
            piece = j * (up_all.shape[1] // 8) + part
            row, col = 8 * (piece % 2), 128 * (piece // 2)
            up_out[row : row + 8, col : col + 128] = up_all[j, 8 * part : 8 * part + 8, :]

    def drain(buffer, semaphore, sent):
        def one(step, carry):
            pltpu.make_async_copy(buffer, buffer, semaphore).wait()
            return carry

        lax.fori_loop(0, sent, one, 0)

    passed = chips // 2 - 1 - outer + outer + 1 - inner
    drain(kv_all.at[chip], block_send.at[0], passed)
    drain(up_part.at[0], sems.at[0], up_pieces - up_owner.astype(jnp.int32))
    drain(ga_part.at[0], sems.at[2], ga_owners - ga_owner.astype(jnp.int32))
    drain(up_sum, sems.at[4], jnp.where(up_owner, ctx_count - 1, 0))
    drain(ga_sum, sems.at[6], jnp.where(ga_owner, total - 1, 0))


def rope_tables(place, tokens):
    positions = (place * tokens + jnp.arange(tokens, dtype=jnp.int32)).astype(F32)
    half = HEAD_SIZE // 2
    freqs = jnp.exp(jnp.arange(half, dtype=F32) * (-2.0 * math.log(ROPE_BASE) / HEAD_SIZE))
    order = jnp.transpose(freqs.reshape(8, 8), (1, 0)).reshape(half)
    angle = order[:, None] * positions[None, :]
    return jnp.cos(angle), jnp.sin(angle)


def on_device(
    counts, layer_input, gain, codes, column_scale_quantized, block_second_scale,
    query_down_map, query_up_map, token_document, output_cotangent,
):
    ctx_count, fsdp_count = counts
    total = ctx_count * fsdp_count
    chips = ctx_count // 2
    rows, width = layer_input.shape
    tokens = 2 * rows
    cos_t, sin_t = rope_tables(lax.axis_index("ctx") // 2, tokens)
    vm = pl.BlockSpec(memory_space=pltpu.VMEM)
    blocks = column_scale_quantized.shape[0]
    rank, local_columns = query_up_map.shape
    heads = local_columns // HEAD_SIZE // 2
    ga_owners = math.gcd(total, width // 128)
    up_pieces = 2 * heads
    vmem, dma = pltpu.VMEM, pltpu.SemaphoreType.DMA
    attn, ga, up = pl.pallas_call(
        functools.partial(step_kernel, counts),
        out_shape=(
            jax.ShapeDtypeStruct(output_cotangent.shape, BF16),
            jax.ShapeDtypeStruct((rank, width), F32),
            jax.ShapeDtypeStruct(query_up_map.shape, F32),
        ),
        in_specs=[vm] * 11,
        out_specs=(vm,) * 3,
        scratch_shapes=[
            vmem((24, blocks, 128), F32),
            vmem((8, blocks // 2, 128), F32),
            vmem((2, tokens, 1024), F32),
            vmem((8, 128, tokens), F32),
            vmem((tokens, width), BF16),
            vmem((8, 32, tokens), F32),
            vmem((8, 32, tokens), BF16),
            vmem((8, 32, tokens), BF16),
            vmem((8, 16 * heads, tokens), F32),
            vmem((8, 16 * heads, tokens), BF16),
            vmem((8, 16 * heads, tokens), BF16),
            vmem((tokens, heads * 128), BF16),
            vmem((16, tokens), BF16),
            vmem((chips, tokens + 16, 256), BF16),
            vmem((256, heads * tokens), BF16),
            vmem((128, heads * tokens), BF16),
            vmem((256 + 16, tokens), BF16),
            vmem((8 * heads, tokens), F32),
            vmem((heads, 256 + 16, tokens), F32),
            vmem((heads, 128 + 16, tokens), F32),
            vmem((8, 128), F32),
            vmem((tokens, heads * 128), BF16),
            vmem((rows, heads * 128), BF16),
            vmem((ga_owners, rank, 128), BF16),
            vmem((total, rank, 128), BF16),
            vmem((rank, 128), BF16),
            vmem((ga_owners, rank, 128), BF16),
            vmem((up_pieces, 8, 128), F32),
            vmem((chips, 8, 128), F32),
            vmem((8, 128), F32),
            vmem((2 * up_pieces, 8, 128), F32),
            dma((6,)),
            dma((6,)),
            dma((1,)),
            dma((chips,)),
            dma((8,)),
        ],
        compiler_params=pltpu.CompilerParams(
            collective_id=0, has_side_effects=True, vmem_limit_bytes=60 * 1024 * 1024
        ),
        name="step",
    )(
        layer_input, gain[None, :], codes, column_scale_quantized, block_second_scale[:, None],
        query_down_map.T, query_up_map, token_document[None, :], cos_t, sin_t, output_cotangent,
    )
    return attn, ga.T, up


def solution(mesh):
    return jax.shard_map(
        functools.partial(on_device, (mesh.shape["ctx"], mesh.shape["fsdp"])),
        mesh=mesh,
        in_specs=(
            P("ctx", None),
            P(),
            P("fsdp", None),
            P("fsdp", None),
            P(),
            P(),
            P(None, "fsdp"),
            P("ctx"),
            P("ctx", "fsdp"),
        ),
        out_specs=(P("ctx", "fsdp"), P(), P(None, "fsdp")),
        check_vma=False,
    )
```

time: 334 us -> 69.5 us (0.21)
  waiting for transfers between devices: 275 us -> 0 us
  Pallas kernels: 36 us -> 61.4 us
  between operations: 13.8 us -> 0.66 us
    psum x2 -> x0, waiting for transfers between devices: 233 us -> none  [the longest x1 134 us: on_device(): ga = lax.psum(ga, ('ctx', 'fsdp'))]
    all_gather x1 -> x0, waiting for transfers between devices: 41.1 us -> none  [on_device(): all_kv = lax.all_gather(kv, 'ctx', axis=0, tiled=False)]
    pallas_call x2 -> x1, Pallas kernels: 36 us -> 61.4 us  [on_device(): pl.pallas_call(functools.partial(step_kernel, counts), out_shape=(jax.Sha...]
  transfers between devices with their start and end apart: 3 -> 0, of which waited for: 3 -> 0; matrix products, arithmetic and copies ran while one was open for 1% -> 0% of each run, Pallas kernels for 0% -> 0%
where the time goes in v2:
time: 69.5 us; the launch traced here: 69.3 us
  Pallas kernels  61.4 us (88%)
  local copies, waits for them, and re-layouts  6.26 us (9%)
  other arithmetic  0.98 us (1%)
    pallas_call x1, Pallas kernels, on_device(): pl.pallas_call(functools.partial(step_kernel, counts), out_shape=(jax.Sha...  61.4 us
    unnamed x3, local copies, waits for them, and re-layouts  4.81 us

profile of v2, /device:TPU:0, one launch (start us, length us, event | category | flops | bytes accessed | tf_op | source)
XLA Modules:
  0.0 69.3 jit_solution(4792538986705637115)
XLA Ops:
  0.7 0.1 exp.10
  0.8 1.4 %copy.12.bss_ref = f32[64,1]{1,0:T(8,128)} copy(f32[64,1]{0,1:T(1,128)} %bitcast.8) | data formatting | bytes 512 | tf_op jit(solution)/shard_map/broadcast_in_dim | solution.py:598
  2.1 1.0 %multiply_sine_fusion = (f32[64,256]{1,0:T(8,128)}, f32[64,256]{1,0:T(8,128)}) fusion(f32[256]{0:T(256)S(1)} %add_convert_fusion, f32[64]{0:T(128)S(1)} %exp.10), kind=kLoop, calls=%fused_computation | loop fusion | flops 16384 | bytes 132352 | tf_op jit(solution)/shard_map/sin | solution.py:526
  3.1 61.4 %step.1 = (bf16[128,1024]{1,0:T(8,128)(2,1)}, f32[16,4096]{1,0:T(8,128)}, f32[16,1024]{1,0:T(8,128)}) custom-call(bf16[128,4096]{1,0:T(8,128)(2,1)} %x_ref.1, f32[1,4096]{1,0:T(1,128)} %bitcast.7, s32[2048,384]{1,0:T(8,128)} %codes_ref.1, s32[32,3072]{1,0:T(8,128)} %cs_ref.1, f32[64,1]{1,0:T(8,128)} %copy.12.bss_ref, bf16[16,4096]{1,0:T(8,128)(2,1)} %bitcast.6, ...), custom_call_target="tpu_custom_call" | custom-call | tf_op jit(solution)/shard_map/step/pallas_call | solution.py:546
  64.5 1.7 %copy.16 = bf16[128,1024]{1,0:T(8,128)(2,1)} copy(bf16[128,1024]{1,0:T(8,128)(2,1)} %get-tuple-element.14) | data formatting | bytes 524288
  66.2 1.7 %copy.17 = f32[4096,16]{0,1:T(8,128)} copy(f32[4096,16]{0,1:T(8,128)} %bitcast.5) | data formatting | bytes 524288
  67.8 1.5 %copy.18 = f32[16,1024]{1,0:T(8,128)} copy(f32[16,1024]{1,0:T(8,128)} %get-tuple-element.16) | data formatting | bytes 131072
  (2 shorter events, 0.0 us)

commit v3 on v2

--- a/solution.py
+++ b/solution.py
@@ -40,6 +40,20 @@
     return jnp.take_along_axis(values, index, axis=1, mode="promise_in_bounds")
 
 
+GATHERED = (1, 3, 5, 7)
+LANE_PICK = lax.GatherDimensionNumbers(
+    offset_dims=(), collapsed_slice_dims=(1,), start_index_map=(1,),
+    operand_batching_dims=(0,), start_indices_batching_dims=(0,),
+)
+
+
+def pick_lanes(values, index):
+    return lax.gather(
+        values, index[..., None], LANE_PICK, (1, 1),
+        mode=lax.GatherScatterMode.PROMISE_IN_BOUNDS,
+    )
+
+
 def dot(a, b):
     return jnp.dot(a, b, preferred_element_type=F32)
 
@@ -60,15 +74,26 @@
 
 def step_kernel(
     counts,
-    x_ref, gain_ref, codes_ref, cs_ref, bss_ref, qdown_ref, qup_ref, ids_ref, cos_ref, sin_ref,
-    do_ref,
+    x_hbm, gain_hbm, codes_hbm, cs_hbm, bss_hbm, qdown_hbm, qup_hbm, ids_hbm, do_hbm,
     out_ref, ga_out, up_out,
-    scl, vscl, acc, acct, xn, own_kv, send_kv, recv_kv, own_q, send_q, recv_q,
-    do_all, ids_all, kv_all, queries, cotans, vk, row_max, out_acc, grad_acc, lin,
-    out_stage, out_in,
+    x_ref, gain_ref, codes_ref, cs_ref, bss_ref, qdown_ref, qup_ref, ids_ref, do_ref, scl, vscl, acc, acct, xn, cos_ref, sin_ref, own_kv, send_kv, recv_kv, own_q, send_q, recv_q,
+    do_all, ids_own, ids_all, kv_all, queries, cotans, vk, row_max, out_acc, grad_acc, lin,
+    out_stage, out_in, mid_own, mid_in,
     ga_part, ga_in, ga_sum, ga_all, up_part, up_in, up_sum, up_all,
-    pair_send, pair_recv, block_send, block_recv, sems,
+    load, pair_send, pair_recv, block_send, block_recv, sems,
 ):
+    loads = [
+        pltpu.make_async_copy(src, dst, load.at[number])
+        for number, (src, dst) in enumerate(
+            (
+                (x_hbm, x_ref), (gain_hbm, gain_ref), (ids_hbm, ids_ref), (do_hbm, do_ref),
+                (bss_hbm, bss_ref), (cs_hbm, cs_ref), (codes_hbm, codes_ref),
+                (qdown_hbm, qdown_ref), (qup_hbm, qup_ref),
+            )
+        )
+    ]
+    for copy in loads:
+        copy.start()
     ctx_count, fsdp_count = counts
     total = ctx_count * fsdp_count
     ctx, member = lax.axis_index("ctx"), lax.axis_index("fsdp")
@@ -100,18 +125,21 @@
 
     mine_at = pl.multiple_of(core * rows, rows)
     other_at = pl.multiple_of((1 - core) * rows, rows)
+    for copy in loads[:3]:
+        copy.wait()
     for r in range(0, rows, 16):
         wide = x_ref[r : r + 16, :].astype(F32)
         inverse = lax.rsqrt(jnp.mean(wide * wide, axis=-1, keepdims=True) + 1e-05)
         xn[pl.ds(pl.multiple_of(mine_at + r, 16), 16), :] = (
             wide * inverse * gain_ref[...]
         ).astype(BF16)
-    ids_all[:, pl.ds(mine_at, rows)] = jnp.broadcast_to(
+    ids_own[...] = jnp.broadcast_to(
         ids_ref[...].astype(F32), (16, rows)
     ).astype(BF16)
     half_columns = do_ref.shape[1] // 2
     mine_columns = pl.multiple_of(core * half_columns, 128)
     other_columns = pl.multiple_of((1 - core) * half_columns, 128)
+    loads[3].wait()
     do_all[pl.ds(mine_at, rows), :] = do_ref[:, pl.ds(mine_columns, half_columns)]
 
     pl.semaphore_wait(barrier, total - 1)
@@ -128,13 +156,38 @@
     beside = (ctx, partner)
     span = pl.ds(mine_at, rows)
     copy_x = pair_copy(xn.at[span], xn.at[span], 0, across)
-    copy_ids = pair_copy(ids_all.at[:, span], ids_all.at[:, span], 1, across)
     copy_do = pair_copy(
         do_ref.at[:, pl.ds(other_columns, half_columns)], do_all.at[span], 2, across
     )
 
+    def send(src, dst, number, ctx_to, fsdp_to):
+        pltpu.make_async_remote_copy(
+            src_ref=src, dst_ref=dst, send_sem=sems.at[2 * number],
+            recv_sem=sems.at[2 * number + 1], device_id=(ctx_to, fsdp_to),
+            device_id_type=MESH,
+        ).start()
+
+    def hold(src, dst, number):
+        pltpu.make_async_copy(src, dst, sems.at[2 * number + 1]).start()
+
+    def await_all(buffer, number):
+        pltpu.make_async_copy(buffer, buffer, sems.at[2 * number + 1]).wait()
+
+    def tell_ids(step, carry):
+        send(ids_own, ids_all.at[chip, :, span], 4, lax.rem(ctx + step, ctx_count), member)
+        return carry
+
+    lax.fori_loop(1, ctx_count, tell_ids, 0)
+
     lane = lax.broadcasted_iota(jnp.int32, (blocks, 128), 1)
-    second = bss_ref[pl.ds(pl.multiple_of(member * blocks, 8), blocks), :]
+    loads[4].wait()
+    loads[5].wait()
+    all_blocks = bss_ref.shape[1]
+    scale_row = lax.broadcasted_iota(jnp.int32, (blocks, all_blocks), 0) + member * blocks
+    scale_lane = lax.broadcasted_iota(jnp.int32, (blocks, all_blocks), 1)
+    second = jnp.sum(
+        jnp.where(scale_row == scale_lane, bss_ref[...], 0.0), axis=1, keepdims=True
+    )
     for tile in range(3):
         source = [
             (cs_ref[:, tile * 1024 + m * 128 : tile * 1024 + (m + 1) * 128].astype(F32) + 1.0)
@@ -149,6 +202,13 @@
                 picked = jnp.where(lane // 16 == m, take_lanes(source[m], index), picked)
             scl[tile * 8 + n] = picked
 
+    at = lax.broadcasted_iota(jnp.int32, (64, tokens), 0)
+    feature = (8 * (at % 8) + at // 8).astype(F32)
+    position = (lax.broadcasted_iota(jnp.int32, (64, tokens), 1) + chip * tokens).astype(F32)
+    angle = position * jnp.exp(feature * (-2.0 * math.log(ROPE_BASE) / HEAD_SIZE))
+    cos_ref[...] = jnp.cos(angle)
+    sin_ref[...] = jnp.sin(angle)
+
     pr = lax.broadcasted_iota(jnp.int32, (128, 128), 0)
     pd = lax.broadcasted_iota(jnp.int32, (128, 128), 1)
     perm = (pd == 8 * (pr % 16) + pr // 16).astype(F32).astype(BF16)
@@ -160,6 +220,9 @@
     half_lane = lax.broadcasted_iota(jnp.int32, (half_blocks, 128), 1)
     long_lane = lax.broadcasted_iota(jnp.int32, (tokens, 128), 1)
     levels = [jnp.full((block_rows, 128), level, BF16) for level in NF4_LEVELS]
+    table = jnp.zeros((block_rows, 128), F32)
+    for code, level in enumerate(NF4_LEVELS):
+        table = jnp.where(short_lane % 16 == code, F32(level), table)
 
     def phase(paired, tile, half):
         if paired:
@@ -199,7 +262,7 @@
             at = pl.multiple_of(member * depth + k * chunk, 128)
             lower = xn[:, pl.ds(at, chunk)]
             upper = xn[:, pl.ds(pl.multiple_of(at + half_depth, 128), chunk)]
-            low_words, high_words = [], []
+            low_words, high_words, full_words = [], [], []
             for b in range(per_chunk):
                 row = pl.multiple_of(k * chunk + b * block_rows, block_rows)
                 words = jnp.where(
@@ -207,6 +270,7 @@
                     words_at(row),
                     pltpu.roll(words_at(pl.multiple_of(row + half_depth, block_rows)), shift, 1),
                 )
+                full_words.append(words)
                 low_words.append(words.astype(I16))
                 high_words.append(jnp.right_shift(words, 16).astype(I16))
             for pair in range(4):
@@ -214,6 +278,11 @@
                 for n in (2 * pair, 2 * pair + 1):
                     pieces = []
                     for b in range(per_chunk):
+                        scale = vscl[n, pl.ds(k * per_chunk + b, 1), :]
+                        if n % 8 in GATHERED:
+                            code = jnp.bitwise_and(jnp.right_shift(full_words[b], 4 * n), 15)
+                            pieces.append((pick_lanes(table, code) * scale).astype(BF16))
+                            continue
                         words = low_words[b] if n < 4 else high_words[b]
                         values = levels
                         for bit in range(4):
@@ -224,7 +293,6 @@
                                 jnp.where(mask, values[v + 1], values[v])
                                 for v in range(0, len(values), 2)
                             ]
-                        scale = vscl[n, pl.ds(k * per_chunk + b, 1), :]
                         pieces.append(values[0] * scale.astype(BF16))
                     planes.append(jnp.concatenate(pieces, axis=0))
                 weight = jnp.concatenate(planes, axis=1)
@@ -239,9 +307,8 @@
             columns = slice(n * 128, (n + 1) * 128)
             acct[n] = jnp.where(keep, acc[0, :, columns], acc[1, :, columns]).T
 
+    loads[6].wait()
     copy_x.wait()
-    copy_ids.wait()
-    copy_do.wait()
 
     def kv_field(group, part):
         at = pl.multiple_of(64 * group, 64) + 32 * part
@@ -261,49 +328,13 @@
     send_q[...] = (acct[:, :64, :] + acct[:, 64:, :]).astype(BF16)
     copy_q = pair_copy(send_q, recv_q, 4, beside)
 
-    place = 3 * member + core
-    phase(False, place // 2, lax.rem(place, 2))
-    own_q[...] = acct[:, :64, :] + acct[:, 64:, :]
-
-    cosine = cos_ref[...].reshape(8, 8, tokens)
-    sine = sin_ref[...].reshape(8, 8, tokens)
-
-    def rotate(field):
-        a, b = field[:, :8, :], field[:, 8:, :]
-        return jnp.concatenate([a * cosine - b * sine, b * cosine + a * sine], axis=1)
-
-    copy_kv.wait()
-    key = own_kv[:, :16, :] + recv_kv[:, :16, :].astype(F32)
-    value = own_kv[:, 16:, :] + recv_kv[:, 16:, :].astype(F32)
-    fields = jnp.concatenate(
-        [value.reshape(128, tokens).astype(BF16), rotate(key).reshape(128, tokens).astype(BF16)],
-        axis=0,
-    )
-    kv_all[chip, :tokens, :] = tn(fields, eye_wide).astype(BF16)
-    kv_all[chip, tokens:, :] = ids_all[...]
-
-    def send_block(block, to_chip):
-        pltpu.make_async_remote_copy(
-            src_ref=kv_all.at[block], dst_ref=kv_all.at[block],
-            send_sem=block_send.at[0], recv_sem=block_recv.at[block],
-            device_id=(2 * to_chip + core, member), device_id_type=MESH,
-        ).start()
-
-    def await_block(block):
-        pltpu.make_async_copy(kv_all.at[block], kv_all.at[block], block_recv.at[block]).wait()
-
-    @pl.when(inner == 0)
-    def _():
-        send_block(chip, chip + 1)
-
-    def along(step, carry):
-        send_block(chip, chip + 2 * step)
-        return carry
-
-    lax.fori_loop(1, chips // 2 - outer, along, 0)
-
+    loads[7].wait()
+    loads[8].wait()
     lr_t = nt(qdown_ref[...], xn[...]).astype(BF16)
-    my_ids = ids_all[...]
+    copy_do.wait()
+    hold(ids_own, ids_all.at[chip, :, span], 4)
+    await_all(ids_all, 4)
+    my_ids = ids_all[chip]
     heads = own_q.shape[1] // 16
     local = pl.multiple_of(core * heads * 128, 128)
     marks = lax.broadcasted_iota(jnp.int32, (128, tokens), 0).astype(F32)
@@ -314,6 +345,46 @@
         queries[128:, columns] = tags
         cotans[:, columns] = nt(perm, do_all[:, head * 128 : (head + 1) * 128]).astype(BF16)
 
+    cosine = cos_ref[...].reshape(8, 8, tokens)
+    sine = sin_ref[...].reshape(8, 8, tokens)
+
+    def rotate(field):
+        a, b = field[:, :8, :], field[:, 8:, :]
+        return jnp.concatenate([a * cosine - b * sine, b * cosine + a * sine], axis=1)
+
+    copy_kv.wait()
+    key = own_kv[:, :16, :] + recv_kv[:, :16, :].astype(F32)
+    value = own_kv[:, 16:, :] + recv_kv[:, 16:, :].astype(F32)
+    fields = jnp.concatenate(
+        [value.reshape(128, tokens).astype(BF16), rotate(key).reshape(128, tokens).astype(BF16)],
+        axis=0,
+    )
+    kv_all[chip] = tn(fields, eye_wide).astype(BF16)
+
+    def send_block(block, to_chip):
+        pltpu.make_async_remote_copy(
+            src_ref=kv_all.at[block], dst_ref=kv_all.at[block],
+            send_sem=block_send.at[0], recv_sem=block_recv.at[block],
+            device_id=(2 * to_chip + core, member), device_id_type=MESH,
+        ).start()
+
+    def await_block(block):
+        pltpu.make_async_copy(kv_all.at[block], kv_all.at[block], block_recv.at[block]).wait()
+
+    @pl.when(inner == 0)
+    def _():
+        send_block(chip, chip + 1)
+
+    def along(step, carry):
+        send_block(chip, chip + 2 * step)
+        return carry
+
+    lax.fori_loop(1, chips // 2 - outer, along, 0)
+
+    place = 3 * member + core
+    phase(False, place // 2, lax.rem(place, 2))
+    own_q[...] = acct[:, :64, :] + acct[:, 64:, :]
+
     copy_q.wait()
     for head in range(heads):
         columns = slice(head * tokens, (head + 1) * tokens)
@@ -333,8 +404,8 @@
     vk[256:, :] = jnp.ones((16, tokens), BF16)
 
     def attend(block, diagonal):
-        both = kv_all[block, :tokens, :]
-        block_ids = kv_all[block, tokens:, :].astype(F32)
+        both = kv_all[block]
+        block_ids = ids_all[block].astype(F32)
         barred = jnp.where(block_ids == tag_row, 0.0, -1e30).astype(BF16)
         barred = tn(barred, spread_tags).astype(BF16)
         lhs = jnp.concatenate([both[:, 128:], barred], axis=1)
@@ -392,16 +463,6 @@
     lax.fori_loop(0, chip, visit, 0)
 
     middle = jnp.zeros((16, tokens), F32)
-    back = 16 * (pd % 8) + pd // 8
-    for head in range(heads):
-        inverse = 1.0 / out_acc[head, 256:257, :]
-        out = (out_acc[head, :128, :] * inverse).astype(BF16)
-        out_stage[:, head * 128 : (head + 1) * 128] = tn(out, perm).astype(BF16)
-    mine_out = pl.ds(mine_at, rows)
-    copy_out = pair_copy(out_stage.at[pl.ds(other_at, rows)], out_in, 5, across)
-    out_ref[:, pl.ds(mine_columns, half_columns)] = out_stage[mine_out, :]
-    up_owners = up_part.shape[0]
-    half_up = up_owners // 2
     for head in range(heads):
         inverse = 1.0 / out_acc[head, 256:257, :]
         mean_dot = grad_acc[head, 128:129, :] * inverse
@@ -410,97 +471,113 @@
         a, b = grad[:, :8, :], grad[:, 8:, :]
         turned = jnp.concatenate([a * cosine + b * sine, b * cosine - a * sine], axis=1)
         lin_t = turned.reshape(128, tokens).astype(BF16)
+        lin[head] = lin_t
         up_cols = qup_ref[:, pl.ds(pl.multiple_of(local + head * 128, 128), 128)]
         middle = middle + dot(nt(up_cols, perm).astype(BF16), lin_t)
-        up = take_lanes(ADAPTER_SCALE * nt(lr_t, lin_t), back[:16])
+    mid_own[...] = middle
+    quarter = 2 * core + member
+    mid_copies = [
+        pair_copy(mid_own, mid_in.at[number], 6 + number, device)
+        for number, device in enumerate(((ctx, partner), (sibling, partner), (sibling, member)))
+    ]
+
+    up_pieces = up_part.shape[0]
+    up_stride = chips // up_pieces
+    up_mine = chip // up_stride
+    owner = lax.rem(chip, up_stride) == 0
+    up_slot = core * up_pieces + up_mine
+    ga_slot = quarter * up_pieces + up_mine
+    low = chip < chips // 2
+
+    def far_first(step, count):
+        return jnp.where(low, count - 1 - step, step)
+
+    back = 16 * (pd % 8) + pd // 8
+    for head in range(heads):
+        up = take_lanes(ADAPTER_SCALE * nt(lr_t, lin[head]), back[:16])
         up_part[2 * head] = up[:8]
         up_part[2 * head + 1] = up[8:]
+
+    def scatter(part, into, number):
+        def one(step, carry):
+            j = far_first(step, up_pieces)
+            to = j * up_stride
+
+            @pl.when(to != chip)
+            def _():
+                send(part.at[j], into.at[chip], number, 2 * to + core, member)
+
+            return carry
+
+        lax.fori_loop(0, up_pieces, one, 0)
+
+        @pl.when(owner)
+        def _():
+            hold(part.at[up_mine], into.at[chip], number)
+
+    scatter(up_part, up_in, 0)
+
+    for head in range(heads):
+        inverse = 1.0 / out_acc[head, 256:257, :]
+        out = (out_acc[head, :128, :] * inverse).astype(BF16)
+        out_stage[:, head * 128 : (head + 1) * 128] = tn(out, perm).astype(BF16)
+
+    for copy in mid_copies:
+        copy.wait()
+    middle = mid_own[...] + mid_in[0] + mid_in[1] + mid_in[2]
     middle = (ADAPTER_SCALE * middle).astype(BF16)
-    ga_owners = ga_part.shape[0]
-    for j in range(ga_owners):
-        ga_part[j] = dot(middle, xn[:, j * 128 : (j + 1) * 128]).astype(BF16)
-
-    up_pieces = up_part.shape[0]
-    up_stride, ga_stride = chips // up_pieces, total // ga_owners
-    up_mine, ga_mine = chip // up_stride, me // ga_stride
-    up_owner, ga_owner = lax.rem(chip, up_stride) == 0, lax.rem(me, ga_stride) == 0
-    up_slot = core * up_pieces + up_mine
-
-    def send(src, dst, number, ctx_to, fsdp_to):
-        pltpu.make_async_remote_copy(
-            src_ref=src, dst_ref=dst, send_sem=sems.at[2 * number],
-            recv_sem=sems.at[2 * number + 1], device_id=(ctx_to, fsdp_to),
-            device_id_type=MESH,
-        ).start()
-
-    def hold(src, dst, number):
-        pltpu.make_async_copy(src, dst, sems.at[2 * number + 1]).start()
-
-    def await_all(buffer, number):
-        pltpu.make_async_copy(buffer, buffer, sems.at[2 * number + 1]).wait()
-
-    def scatter_up(step, carry):
-        j = lax.rem(up_mine + step, up_pieces)
-        to = j * up_stride
-
-        @pl.when(to != chip)
-        def _():
-            send(up_part.at[j], up_in.at[chip], 0, 2 * to + core, member)
-
-        return carry
-
-    def scatter_ga(step, carry):
-        j = lax.rem(ga_mine + step, ga_owners)
-        to = j * ga_stride
-
-        @pl.when(to != me)
-        def _():
-            send(ga_part.at[j], ga_in.at[me], 1, to // fsdp_count, lax.rem(to, fsdp_count))
-
-        return carry
-
-    lax.fori_loop(0, ga_owners, scatter_ga, 0)
-    lax.fori_loop(0, up_pieces, scatter_up, 0)
+    share = up_pieces * 128
+    ga = dot(middle, xn[:, pl.ds(pl.multiple_of(quarter * share, 128), share)])
+    for j in range(up_pieces):
+        ga_part[j] = ga[:, j * 128 : (j + 1) * 128].astype(BF16)
+    scatter(ga_part, ga_in, 1)
+
+    copy_out = pair_copy(out_stage.at[pl.ds(other_at, rows)], out_in, 5, across)
+    out_ref[:, pl.ds(mine_columns, half_columns)] = out_stage[pl.ds(mine_at, rows), :]
+
+    @pl.when(owner)
+    def _():
+        await_all(up_in, 0)
+        up_sum[...] = jnp.sum(up_in[...], axis=0)
+
+        def spread_up(step, carry):
+            to = far_first(step, ctx_count)
+
+            @pl.when(to != ctx)
+            def _():
+                send(up_sum, up_all.at[up_slot], 2, to, member)
+
+            return carry
+
+        lax.fori_loop(0, ctx_count, spread_up, 0)
+        hold(up_sum, up_all.at[up_slot], 2)
+
+        await_all(ga_in, 1)
+        ga_sum[...] = jnp.sum(ga_in[...].astype(F32), axis=0).astype(BF16)
+
+        def spread_ga(step, carry):
+            place = far_first(step, total)
+            to, to_fsdp = place // fsdp_count, lax.rem(place, fsdp_count)
+
+            @pl.when(place != me)
+            def _():
+                send(ga_sum, ga_all.at[ga_slot], 3, to, to_fsdp)
+
+            return carry
+
+        lax.fori_loop(0, total, spread_ga, 0)
+        hold(ga_sum, ga_all.at[ga_slot], 3)
 
     copy_out.wait()
     out_ref[:, pl.ds(other_columns, half_columns)] = out_in[...]
 
-    @pl.when(ga_owner)
-    def _():
-        hold(ga_part.at[ga_mine], ga_in.at[me], 1)
-        await_all(ga_in, 1)
-        ga_sum[...] = jnp.sum(ga_in[...].astype(F32), axis=0).astype(BF16)
-
-        def spread(step, carry):
-            to = lax.rem(me + step, total)
-            send(ga_sum, ga_all.at[ga_mine], 3, to // fsdp_count, lax.rem(to, fsdp_count))
-            return carry
-
-        lax.fori_loop(1, total, spread, 0)
-        hold(ga_sum, ga_all.at[ga_mine], 3)
-
-    @pl.when(up_owner)
-    def _():
-        hold(up_part.at[up_mine], up_in.at[chip], 0)
-        await_all(up_in, 0)
-        up_sum[...] = jnp.sum(up_in[...], axis=0)
-
-        def spread(step, carry):
-            send(up_sum, up_all.at[up_slot], 2, lax.rem(ctx + step, ctx_count), member)
-            return carry
-
-        lax.fori_loop(1, ctx_count, spread, 0)
-        hold(up_sum, up_all.at[up_slot], 2)
-
-    await_all(ga_all, 3)
-    for j in range(ga_owners):
-        ga_out[:, j * 128 : (j + 1) * 128] = ga_all[j].astype(F32)
     await_all(up_all, 2)
     for j in range(2 * up_pieces):
-        for part in range(up_all.shape[1] // 8):
-            piece = j * (up_all.shape[1] // 8) + part
-            row, col = 8 * (piece % 2), 128 * (piece // 2)
-            up_out[row : row + 8, col : col + 128] = up_all[j, 8 * part : 8 * part + 8, :]
+        row, col = 8 * (j % 2), 128 * (j // 2)
+        up_out[row : row + 8, col : col + 128] = up_all[j]
+    await_all(ga_all, 3)
+    for j in range(4 * up_pieces):
+        ga_out[:, j * 128 : (j + 1) * 128] = ga_all[j].astype(F32)
 
     def drain(buffer, semaphore, sent):
         def one(step, carry):
@@ -511,19 +588,12 @@
 
     passed = chips // 2 - 1 - outer + outer + 1 - inner
     drain(kv_all.at[chip], block_send.at[0], passed)
-    drain(up_part.at[0], sems.at[0], up_pieces - up_owner.astype(jnp.int32))
-    drain(ga_part.at[0], sems.at[2], ga_owners - ga_owner.astype(jnp.int32))
-    drain(up_sum, sems.at[4], jnp.where(up_owner, ctx_count - 1, 0))
-    drain(ga_sum, sems.at[6], jnp.where(ga_owner, total - 1, 0))
-
-
-def rope_tables(place, tokens):
-    positions = (place * tokens + jnp.arange(tokens, dtype=jnp.int32)).astype(F32)
-    half = HEAD_SIZE // 2
-    freqs = jnp.exp(jnp.arange(half, dtype=F32) * (-2.0 * math.log(ROPE_BASE) / HEAD_SIZE))
-    order = jnp.transpose(freqs.reshape(8, 8), (1, 0)).reshape(half)
-    angle = order[:, None] * positions[None, :]
-    return jnp.cos(angle), jnp.sin(angle)
+    scattered = up_pieces - owner.astype(jnp.int32)
+    drain(up_part.at[0], sems.at[0], scattered)
+    drain(ga_part.at[0], sems.at[2], scattered)
+    drain(up_sum, sems.at[4], jnp.where(owner, ctx_count - 1, 0))
+    drain(ga_sum, sems.at[6], jnp.where(owner, total - 1, 0))
+    drain(ids_own, sems.at[8], ctx_count - 1)
 
 
 def on_device(
@@ -535,29 +605,39 @@
     chips = ctx_count // 2
     rows, width = layer_input.shape
     tokens = 2 * rows
-    cos_t, sin_t = rope_tables(lax.axis_index("ctx") // 2, tokens)
     vm = pl.BlockSpec(memory_space=pltpu.VMEM)
+    hbm = pl.BlockSpec(memory_space=pltpu.HBM)
     blocks = column_scale_quantized.shape[0]
     rank, local_columns = query_up_map.shape
     heads = local_columns // HEAD_SIZE // 2
-    ga_owners = math.gcd(total, width // 128)
     up_pieces = 2 * heads
     vmem, dma = pltpu.VMEM, pltpu.SemaphoreType.DMA
     attn, ga, up = pl.pallas_call(
         functools.partial(step_kernel, counts),
         out_shape=(
-            jax.ShapeDtypeStruct(output_cotangent.shape, BF16),
-            jax.ShapeDtypeStruct((rank, width), F32),
-            jax.ShapeDtypeStruct(query_up_map.shape, F32),
+            vmem(output_cotangent.shape, BF16),
+            vmem((rank, width), F32),
+            vmem(query_up_map.shape, F32),
         ),
-        in_specs=[vm] * 11,
+        in_specs=[hbm] * 9,
         out_specs=(vm,) * 3,
         scratch_shapes=[
+            vmem(layer_input.shape, BF16),
+            vmem((1, width), F32),
+            vmem(codes.shape, jnp.int32),
+            vmem(column_scale_quantized.shape, jnp.int32),
+            vmem((1, block_second_scale.shape[0]), F32),
+            vmem((rank, width), BF16),
+            vmem(query_up_map.shape, BF16),
+            vmem((1, rows), jnp.int32),
+            vmem(output_cotangent.shape, BF16),
             vmem((24, blocks, 128), F32),
             vmem((8, blocks // 2, 128), F32),
             vmem((2, tokens, 1024), F32),
             vmem((8, 128, tokens), F32),
             vmem((tokens, width), BF16),
+            vmem((HEAD_SIZE // 2, tokens), F32),
+            vmem((HEAD_SIZE // 2, tokens), F32),
             vmem((8, 32, tokens), F32),
             vmem((8, 32, tokens), BF16),
             vmem((8, 32, tokens), BF16),
@@ -565,38 +645,42 @@
             vmem((8, 16 * heads, tokens), BF16),
             vmem((8, 16 * heads, tokens), BF16),
             vmem((tokens, heads * 128), BF16),
-            vmem((16, tokens), BF16),
-            vmem((chips, tokens + 16, 256), BF16),
+            vmem((16, rows), BF16),
+            vmem((chips, 16, tokens), BF16),
+            vmem((chips, tokens, 256), BF16),
             vmem((256, heads * tokens), BF16),
             vmem((128, heads * tokens), BF16),
             vmem((256 + 16, tokens), BF16),
             vmem((8 * heads, tokens), F32),
             vmem((heads, 256 + 16, tokens), F32),
             vmem((heads, 128 + 16, tokens), F32),
-            vmem((8, 128), F32),
+            vmem((heads, 128, tokens), BF16),
             vmem((tokens, heads * 128), BF16),
             vmem((rows, heads * 128), BF16),
-            vmem((ga_owners, rank, 128), BF16),
-            vmem((total, rank, 128), BF16),
+            vmem((rank, tokens), F32),
+            vmem((3, rank, tokens), F32),
+            vmem((up_pieces, rank, 128), BF16),
+            vmem((chips, rank, 128), BF16),
             vmem((rank, 128), BF16),
-            vmem((ga_owners, rank, 128), BF16),
+            vmem((4 * up_pieces, rank, 128), BF16),
             vmem((up_pieces, 8, 128), F32),
             vmem((chips, 8, 128), F32),
             vmem((8, 128), F32),
             vmem((2 * up_pieces, 8, 128), F32),
-            dma((6,)),
-            dma((6,)),
+            dma((9,)),
+            dma((9,)),
+            dma((9,)),
             dma((1,)),
             dma((chips,)),
-            dma((8,)),
+            dma((10,)),
         ],
         compiler_params=pltpu.CompilerParams(
-            collective_id=0, has_side_effects=True, vmem_limit_bytes=60 * 1024 * 1024
+            collective_id=0, has_side_effects=True, vmem_limit_bytes=56 * 1024 * 1024
         ),
         name="step",
     )(
-        layer_input, gain[None, :], codes, column_scale_quantized, block_second_scale[:, None],
-        query_down_map.T, query_up_map, token_document[None, :], cos_t, sin_t, output_cotangent,
+        layer_input, gain[None, :], codes, column_scale_quantized, block_second_scale[None, :],
+        query_down_map.T, query_up_map, token_document[None, :], output_cotangent,
     )
     return attn, ga.T, up
 

time: 69.5 us -> 54.8 us (0.79)
  Pallas kernels: 61.4 us -> 52 us
  local copies, waits for them, and re-layouts: 6.26 us -> 2.04 us
  other arithmetic: 0.98 us -> 0 us
    pallas_call x1, Pallas kernels: 61.4 us -> 52 us  [on_device(): pl.pallas_call(functools.partial(step_kernel, counts), out_shape=(vmem(ou...]
    unnamed x3, local copies, waits for them, and re-layouts: 4.81 us -> 2.04 us
    broadcast_in_dim x1 -> x0, local copies, waits for them, and re-layouts: 1.37 us -> none  [on_device(): block_second_scale[:, None]]
    sin x1 -> x0, other arithmetic: 0.96 us -> none  [rope_tables(): return (jnp.cos(angle), jnp.sin(angle))]
where the time goes in v3:
time: 54.8 us; the launch traced here: 54.7 us
  Pallas kernels  52 us (95%)
  local copies, waits for them, and re-layouts  2.04 us (4%)
  between operations  0.64 us (1%)
    pallas_call x1, Pallas kernels, on_device(): pl.pallas_call(functools.partial(step_kernel, counts), out_shape=(vmem(ou...  52 us
    unnamed x3, local copies, waits for them, and re-layouts  2.04 us

profile of v3, /device:TPU:0, one launch (start us, length us, event | category | flops | bytes accessed | tf_op | source)
XLA Modules:
  0.0 54.7 jit_solution(13262131854645941190)
XLA Ops:
  0.6 52.0 %step.1 = (bf16[128,1024]{1,0:T(8,128)(2,1)S(1)}, f32[16,4096]{1,0:T(8,128)S(1)}, f32[16,1024]{1,0:T(8,128)S(1)}) custom-call(bf16[128,4096]{1,0:T(8,128)(2,1)} %x_hbm.1, f32[1,4096]{1,0:T(1,128)} %bitcast.7, s32[2048,384]{1,0:T(8,128)} %codes_hbm.1, s32[32,3072]{1,0:T(8,128)} %cs_hbm.1, f32[1,64]{1,0:T(1,128)} %bitcast.8, bf16[16,4096]{1,0:T(8,128)(2,1)} %bitcast.6, ...), custom_call_target="tpu_custom_call" | custom-call | tf_op jit(solution)/shard_map/step/pallas_call | solution.py:615
  52.6 0.7 %copy.15 = bf16[128,1024]{1,0:T(8,128)(2,1)} copy(bf16[128,1024]{1,0:T(8,128)(2,1)S(1)} %get-tuple-element.9) | data formatting | bytes 524288
  53.3 0.7 %copy.16 = f32[4096,16]{0,1:T(8,128)} copy(f32[4096,16]{0,1:T(8,128)S(1)} %bitcast.5) | data formatting | bytes 524288
  54.0 0.6 %copy.17 = f32[16,1024]{1,0:T(8,128)} copy(f32[16,1024]{1,0:T(8,128)S(1)} %get-tuple-element.11) | data formatting | bytes 131072

commit v4 on v3

--- a/solution.py
+++ b/solution.py
@@ -78,7 +78,7 @@
     out_ref, ga_out, up_out,
     x_ref, gain_ref, codes_ref, cs_ref, bss_ref, qdown_ref, qup_ref, ids_ref, do_ref, scl, vscl, acc, acct, xn, cos_ref, sin_ref, own_kv, send_kv, recv_kv, own_q, send_q, recv_q,
     do_all, ids_own, ids_all, kv_all, queries, cotans, vk, row_max, out_acc, grad_acc, lin,
-    out_stage, out_in, mid_own, mid_in,
+    score_buf, dots_buf, prob_buf, weight_buf, out_stage, out_in, mid_own, mid_in,
     ga_part, ga_in, ga_sum, ga_all, up_part, up_in, up_sum, up_all,
     load, pair_send, pair_recv, block_send, block_recv, sems,
 ):
@@ -155,7 +155,10 @@
     across = (sibling, member)
     beside = (ctx, partner)
     span = pl.ds(mine_at, rows)
-    copy_x = pair_copy(xn.at[span], xn.at[span], 0, across)
+    near = xn.at[span, pl.ds(pl.multiple_of(member * depth, 128), depth)]
+    far = xn.at[span, pl.ds(pl.multiple_of(partner * depth, 128), depth)]
+    copy_x = pair_copy(near, near, 0, across)
+    copy_x_rest = pair_copy(far, far, 1, across)
     copy_do = pair_copy(
         do_ref.at[:, pl.ds(other_columns, half_columns)], do_all.at[span], 2, across
     )
@@ -317,11 +320,12 @@
         ]
 
     phase(True, 0, 0)
+    copy_kv = [None, None]
+    for part in (1, 0):
+        send_kv[part] = kv_field(partner, part).astype(BF16)
+        copy_kv[part] = pair_copy(send_kv.at[part], recv_kv.at[part], 3 + 6 * part, beside)
     for part in range(2):
-        send_kv[:, 16 * part : 16 * part + 16, :] = kv_field(partner, part).astype(BF16)
-    copy_kv = pair_copy(send_kv, recv_kv, 3, beside)
-    for part in range(2):
-        own_kv[:, 16 * part : 16 * part + 16, :] = kv_field(member, part)
+        own_kv[part] = kv_field(member, part)
 
     place = 3 * partner + core
     phase(False, place // 2, lax.rem(place, 2))
@@ -330,6 +334,7 @@
 
     loads[7].wait()
     loads[8].wait()
+    copy_x_rest.wait()
     lr_t = nt(qdown_ref[...], xn[...]).astype(BF16)
     copy_do.wait()
     hold(ids_own, ids_all.at[chip, :, span], 4)
@@ -352,38 +357,55 @@
         a, b = field[:, :8, :], field[:, 8:, :]
         return jnp.concatenate([a * cosine - b * sine, b * cosine + a * sine], axis=1)
 
-    copy_kv.wait()
-    key = own_kv[:, :16, :] + recv_kv[:, :16, :].astype(F32)
-    value = own_kv[:, 16:, :] + recv_kv[:, 16:, :].astype(F32)
-    fields = jnp.concatenate(
-        [value.reshape(128, tokens).astype(BF16), rotate(key).reshape(128, tokens).astype(BF16)],
-        axis=0,
-    )
-    kv_all[chip] = tn(fields, eye_wide).astype(BF16)
-
-    def send_block(block, to_chip):
+    has_next = outer + 1 < chips // 2
+
+    def send_block(block, part, to_chip):
+        half = kv_all.at[block, part]
         pltpu.make_async_remote_copy(
-            src_ref=kv_all.at[block], dst_ref=kv_all.at[block],
-            send_sem=block_send.at[0], recv_sem=block_recv.at[block],
+            src_ref=half, dst_ref=half,
+            send_sem=block_send.at[0], recv_sem=block_recv.at[2 * block + part],
             device_id=(2 * to_chip + core, member), device_id_type=MESH,
         ).start()
 
-    def await_block(block):
-        pltpu.make_async_copy(kv_all.at[block], kv_all.at[block], block_recv.at[block]).wait()
-
-    @pl.when(inner == 0)
-    def _():
-        send_block(chip, chip + 1)
-
-    def along(step, carry):
-        send_block(chip, chip + 2 * step)
-        return carry
-
-    lax.fori_loop(1, chips // 2 - outer, along, 0)
+    def await_block(block, part):
+        half = kv_all.at[block, part]
+        pltpu.make_async_copy(half, half, block_recv.at[2 * block + part]).wait()
+
+    def relay(ahead):
+        block = 2 * (outer - 1 - ahead) + inner
+        for part in range(2):
+            await_block(block, part)
+
+            @pl.when(has_next)
+            def _():
+                send_block(block, part, chip + 2)
+
+            send_block(block, part, 2 * outer + 1 - inner)
+
+    eye_half = eye(128)
+    for part in (1, 0):
+        copy_kv[part].wait()
+        field = own_kv[part] + recv_kv[part].astype(F32)
+        if part == 0:
+            field = rotate(field)
+        field = field.reshape(128, tokens).astype(BF16)
+        kv_all[chip, 1 - part] = tn(field, eye_half).astype(BF16)
+
+        @pl.when(has_next)
+        def _():
+            send_block(chip, 1 - part, chip + 2)
+
+        @pl.when(inner == 0)
+        def _():
+            send_block(chip, 1 - part, chip + 1)
 
     place = 3 * member + core
     phase(False, place // 2, lax.rem(place, 2))
     own_q[...] = acct[:, :64, :] + acct[:, 64:, :]
+
+    @pl.when(outer > 0)
+    def _():
+        relay(0)
 
     copy_q.wait()
     for head in range(heads):
@@ -404,34 +426,42 @@
     vk[256:, :] = jnp.ones((16, tokens), BF16)
 
     def attend(block, diagonal):
-        both = kv_all[block]
+        both = jnp.concatenate([kv_all[block, 0], kv_all[block, 1]], axis=1)
         block_ids = ids_all[block].astype(F32)
         barred = jnp.where(block_ids == tag_row, 0.0, -1e30).astype(BF16)
         barred = tn(barred, spread_tags).astype(BF16)
         lhs = jnp.concatenate([both[:, 128:], barred], axis=1)
         vk[:256, :] = nt(eye_wide, both).astype(BF16)
+        tops, decays = [], []
         for head in range(heads):
             columns = slice(head * tokens, (head + 1) * tokens)
-            row = slice(8 * head, 8 * head + 1)
             scores = dot(lhs, queries[:, columns]) * log_scale
             if diagonal:
                 ki = lax.broadcasted_iota(jnp.int32, (tokens, tokens), 0)
                 qi = lax.broadcasted_iota(jnp.int32, (tokens, tokens), 1)
                 scores = jnp.where(ki <= qi, scores, -1e30)
-            top = jnp.max(scores, axis=0, keepdims=True)
+            score_buf[head] = scores
+            tops.append(jnp.max(scores, axis=0, keepdims=True))
+            dots_buf[head] = dot(both[:, :128], cotans[:, columns])
+        for head in range(heads):
+            row = slice(8 * head, 8 * head + 1)
+            top = tops[head]
             if not diagonal:
                 before = row_max[row, :]
                 top = jnp.maximum(top, before)
-            expo = jnp.exp2(scores - top)
-            weighted = expo * dot(both[:, :128], cotans[:, columns])
-            new_out = dot(vk[...], expo.astype(BF16))
-            new_grad = dot(vk[128:, :], weighted.astype(BF16))
+                decays.append(jnp.exp2(before - top))
             row_max[row, :] = top
+            expo = jnp.exp2(score_buf[head] - top)
+            prob_buf[head] = expo.astype(BF16)
+            weight_buf[head] = (expo * dots_buf[head]).astype(BF16)
+        for head in range(heads):
+            new_out = dot(vk[...], prob_buf[head])
+            new_grad = dot(vk[128:, :], weight_buf[head])
             if diagonal:
                 out_acc[head] = new_out
                 grad_acc[head] = new_grad
             else:
-                decay = jnp.exp2(before - top)
+                decay = decays[head]
                 out_acc[head] = decay * out_acc[head] + new_out
                 grad_acc[head] = decay * grad_acc[head] + new_grad
 
@@ -442,11 +472,9 @@
         odd = lax.rem(place + 2, 2) == 1
         ahead = (place + 1) // 2
 
-        @pl.when(((step == 0) | odd) & (ahead < outer))
+        @pl.when(odd & (ahead > 0) & (ahead < outer))
         def _():
-            block = 2 * (outer - 1 - ahead) + inner
-            await_block(block)
-            send_block(block, 2 * outer + 1 - inner)
+            relay(ahead)
 
         crossed = 2 * (outer - 1 - (place - 1) // 2) + 1 - inner
         crossed = jnp.where(place < 0, chip - 1, crossed)
@@ -455,7 +483,8 @@
 
         @pl.when(odd)
         def _():
-            await_block(block)
+            await_block(block, 0)
+            await_block(block, 1)
 
         attend(block, False)
         return carry
@@ -586,14 +615,28 @@
 
         lax.fori_loop(0, sent, one, 0)
 
-    passed = chips // 2 - 1 - outer + outer + 1 - inner
-    drain(kv_all.at[chip], block_send.at[0], passed)
+    onward = has_next.astype(jnp.int32)
+    passed = 2 * (onward + 1 - inner + outer * (onward + 1))
+    drain(kv_all.at[chip, 0], block_send.at[0], passed)
     scattered = up_pieces - owner.astype(jnp.int32)
     drain(up_part.at[0], sems.at[0], scattered)
     drain(ga_part.at[0], sems.at[2], scattered)
     drain(up_sum, sems.at[4], jnp.where(owner, ctx_count - 1, 0))
     drain(ga_sum, sems.at[6], jnp.where(owner, total - 1, 0))
     drain(ids_own, sems.at[8], ctx_count - 1)
+
+
+def store_kernel(attn_ref, ga_ref, up_ref, attn_out, ga_out, up_out, sems):
+    copies = [
+        pltpu.make_async_copy(src, dst, sems.at[number])
+        for number, (src, dst) in enumerate(
+            ((attn_ref, attn_out), (ga_ref, ga_out), (up_ref, up_out))
+        )
+    ]
+    for copy in copies:
+        copy.start()
+    for copy in copies:
+        copy.wait()
 
 
 def on_device(
@@ -638,16 +681,16 @@
             vmem((tokens, width), BF16),
             vmem((HEAD_SIZE // 2, tokens), F32),
             vmem((HEAD_SIZE // 2, tokens), F32),
-            vmem((8, 32, tokens), F32),
-            vmem((8, 32, tokens), BF16),
-            vmem((8, 32, tokens), BF16),
+            vmem((2, 8, 16, tokens), F32),
+            vmem((2, 8, 16, tokens), BF16),
+            vmem((2, 8, 16, tokens), BF16),
             vmem((8, 16 * heads, tokens), F32),
             vmem((8, 16 * heads, tokens), BF16),
             vmem((8, 16 * heads, tokens), BF16),
             vmem((tokens, heads * 128), BF16),
             vmem((16, rows), BF16),
             vmem((chips, 16, tokens), BF16),
-            vmem((chips, tokens, 256), BF16),
+            vmem((chips, 2, tokens, 128), BF16),
             vmem((256, heads * tokens), BF16),
             vmem((128, heads * tokens), BF16),
             vmem((256 + 16, tokens), BF16),
@@ -655,6 +698,10 @@
             vmem((heads, 256 + 16, tokens), F32),
             vmem((heads, 128 + 16, tokens), F32),
             vmem((heads, 128, tokens), BF16),
+            vmem((heads, tokens, tokens), F32),
+            vmem((heads, tokens, tokens), F32),
+            vmem((heads, tokens, tokens), BF16),
+            vmem((heads, tokens, tokens), BF16),
             vmem((tokens, heads * 128), BF16),
             vmem((rows, heads * 128), BF16),
             vmem((rank, tokens), F32),
@@ -668,10 +715,10 @@
             vmem((8, 128), F32),
             vmem((2 * up_pieces, 8, 128), F32),
             dma((9,)),
-            dma((9,)),
-            dma((9,)),
+            dma((10,)),
+            dma((10,)),
             dma((1,)),
-            dma((chips,)),
+            dma((2 * chips,)),
             dma((10,)),
         ],
         compiler_params=pltpu.CompilerParams(
@@ -682,6 +729,15 @@
         layer_input, gain[None, :], codes, column_scale_quantized, block_second_scale[None, :],
         query_down_map.T, query_up_map, token_document[None, :], output_cotangent,
     )
+    attn, ga, up = pl.pallas_call(
+        store_kernel,
+        out_shape=tuple(jax.ShapeDtypeStruct(a.shape, a.dtype) for a in (attn, ga, up)),
+        in_specs=[vm] * 3,
+        out_specs=(hbm,) * 3,
+        scratch_shapes=[dma((3,))],
+        compiler_params=pltpu.CompilerParams(vmem_limit_bytes=4 * 1024 * 1024),
+        name="store",
+    )(attn, ga, up)
     return attn, ga.T, up
 
 

time: 54.8 us -> 47.8 us (0.87)
  Pallas kernels: 52 us -> 47 us
  local copies, waits for them, and re-layouts: 2.04 us -> 0 us
    pallas_call x1, Pallas kernels: 52 us -> 46.2 us  [on_device(): pl.pallas_call(functools.partial(step_kernel, counts), out_shape=(vmem(ou...]
    unnamed x3 -> x0, local copies, waits for them, and re-layouts: 2.04 us -> none
    pallas_call x0 -> x1, Pallas kernels: none -> 0.83 us  [on_device(): pl.pallas_call(store_kernel, out_shape=tuple((jax.ShapeDtypeStruct(a.shap...]
where the time goes in v4:
time: 47.8 us; the launch traced here: 47.6 us
  Pallas kernels  47 us (98%)
  between operations  0.64 us (1%)
    pallas_call x1, Pallas kernels, on_device(): pl.pallas_call(functools.partial(step_kernel, counts), out_shape=(vmem(ou...  46.2 us

profile of v4, /device:TPU:0, one launch (start us, length us, event | category | flops | bytes accessed | tf_op | source)
XLA Modules:
  0.0 47.6 jit_solution(18055822053557919789)
XLA Ops:
  0.6 46.2 %step.1 = (bf16[128,1024]{1,0:T(8,128)(2,1)S(1)}, f32[16,4096]{1,0:T(8,128)S(1)}, f32[16,1024]{1,0:T(8,128)S(1)}) custom-call(bf16[128,4096]{1,0:T(8,128)(2,1)} %x_hbm.1, f32[1,4096]{1,0:T(1,128)} %bitcast.6, s32[2048,384]{1,0:T(8,128)} %codes_hbm.1, s32[32,3072]{1,0:T(8,128)} %cs_hbm.1, f32[1,64]{1,0:T(1,128)} %bitcast.7, bf16[16,4096]{1,0:T(8,128)(2,1)} %bitcast.5, ...), custom_call_target="tpu_custom_call" | custom-call | tf_op jit(solution)/shard_map/step/pallas_call | solution.py:658
  46.8 0.8 %store.1 = (bf16[128,1024]{1,0:T(8,128)(2,1)}, f32[16,4096]{1,0:T(8,128)}, f32[16,1024]{1,0:T(8,128)}) custom-call(bf16[128,1024]{1,0:T(8,128)(2,1)S(1)} %get-tuple-element.9.attn_ref, f32[16,4096]{1,0:T(8,128)S(1)} %get-tuple-element.10.ga_ref, f32[16,1024]{1,0:T(8,128)S(1)} %get-tuple-element.11.up_ref), custom_call_target="tpu_custom_call" | custom-call | tf_op jit(solution)/shard_map/store/pallas_call | solution.py:732

commit v5 on v4

--- a/solution.py
+++ b/solution.py
@@ -76,24 +76,26 @@
     counts,
     x_hbm, gain_hbm, codes_hbm, cs_hbm, bss_hbm, qdown_hbm, qup_hbm, ids_hbm, do_hbm,
     out_ref, ga_out, up_out,
-    x_ref, gain_ref, codes_ref, cs_ref, bss_ref, qdown_ref, qup_ref, ids_ref, do_ref, scl, vscl, acc, acct, xn, cos_ref, sin_ref, own_kv, send_kv, recv_kv, own_q, send_q, recv_q,
+    x_ref, gain_ref, codes_ref, cs_ref, bss_ref, qdown_ref, qup_ref, ids_ref, do_ref, scl, vscl, weights, acc, acct, xn, cos_ref, sin_ref, own_kv, send_kv, recv_kv, own_q, send_q, recv_q,
     do_all, ids_own, ids_all, kv_all, queries, cotans, vk, row_max, out_acc, grad_acc, lin,
     score_buf, dots_buf, prob_buf, weight_buf, out_stage, out_in, mid_own, mid_in,
     ga_part, ga_in, ga_sum, ga_all, up_part, up_in, up_sum, up_all,
     load, pair_send, pair_recv, block_send, block_recv, sems,
 ):
+    early = x_hbm.shape[0] // 2
     loads = [
         pltpu.make_async_copy(src, dst, load.at[number])
         for number, (src, dst) in enumerate(
             (
-                (x_hbm, x_ref), (gain_hbm, gain_ref), (ids_hbm, ids_ref), (do_hbm, do_ref),
+                (x_hbm.at[:early], x_ref.at[:early]), (gain_hbm, gain_ref), (ids_hbm, ids_ref),
+                (do_hbm, do_ref),
                 (bss_hbm, bss_ref), (cs_hbm, cs_ref), (codes_hbm, codes_ref),
-                (qdown_hbm, qdown_ref), (qup_hbm, qup_ref),
+                (qdown_hbm, qdown_ref), (qup_hbm, qup_ref), (x_hbm.at[early:], x_ref.at[early:]),
             )
         )
     ]
-    for copy in loads:
-        copy.start()
+    for number in (0, 1, 9, 2, 3, 4, 5, 6, 7, 8):
+        loads[number].start()
     ctx_count, fsdp_count = counts
     total = ctx_count * fsdp_count
     ctx, member = lax.axis_index("ctx"), lax.axis_index("fsdp")
@@ -113,26 +115,38 @@
 
     barrier = pltpu.get_barrier_semaphore()
 
+    low = chip < chips // 2
+
+    def far_first(step, count):
+        return jnp.where(low, count - 1 - step, step)
+
     def greet(step, carry):
-        other = lax.rem(me + step, total)
-        pl.semaphore_signal(
-            barrier, inc=1, device_id=(other // fsdp_count, lax.rem(other, fsdp_count)),
-            device_id_type=MESH,
-        )
+        other = far_first(step, total)
+
+        @pl.when(other != me)
+        def _():
+            pl.semaphore_signal(
+                barrier, inc=1, device_id=(other // fsdp_count, lax.rem(other, fsdp_count)),
+                device_id_type=MESH,
+            )
+
         return carry
 
-    lax.fori_loop(1, total, greet, 0)
+    lax.fori_loop(0, total, greet, 0)
 
     mine_at = pl.multiple_of(core * rows, rows)
     other_at = pl.multiple_of((1 - core) * rows, rows)
-    for copy in loads[:3]:
-        copy.wait()
+    loads[0].wait()
+    loads[1].wait()
     for r in range(0, rows, 16):
+        if r == early:
+            loads[9].wait()
         wide = x_ref[r : r + 16, :].astype(F32)
         inverse = lax.rsqrt(jnp.mean(wide * wide, axis=-1, keepdims=True) + 1e-05)
         xn[pl.ds(pl.multiple_of(mine_at + r, 16), 16), :] = (
             wide * inverse * gain_ref[...]
         ).astype(BF16)
+    loads[2].wait()
     ids_own[...] = jnp.broadcast_to(
         ids_ref[...].astype(F32), (16, rows)
     ).astype(BF16)
@@ -141,46 +155,6 @@
     other_columns = pl.multiple_of((1 - core) * half_columns, 128)
     loads[3].wait()
     do_all[pl.ds(mine_at, rows), :] = do_ref[:, pl.ds(mine_columns, half_columns)]
-
-    pl.semaphore_wait(barrier, total - 1)
-
-    def pair_copy(src, dst, number, device):
-        copy = pltpu.make_async_remote_copy(
-            src_ref=src, dst_ref=dst, send_sem=pair_send.at[number],
-            recv_sem=pair_recv.at[number], device_id=device, device_id_type=MESH,
-        )
-        copy.start()
-        return copy
-
-    across = (sibling, member)
-    beside = (ctx, partner)
-    span = pl.ds(mine_at, rows)
-    near = xn.at[span, pl.ds(pl.multiple_of(member * depth, 128), depth)]
-    far = xn.at[span, pl.ds(pl.multiple_of(partner * depth, 128), depth)]
-    copy_x = pair_copy(near, near, 0, across)
-    copy_x_rest = pair_copy(far, far, 1, across)
-    copy_do = pair_copy(
-        do_ref.at[:, pl.ds(other_columns, half_columns)], do_all.at[span], 2, across
-    )
-
-    def send(src, dst, number, ctx_to, fsdp_to):
-        pltpu.make_async_remote_copy(
-            src_ref=src, dst_ref=dst, send_sem=sems.at[2 * number],
-            recv_sem=sems.at[2 * number + 1], device_id=(ctx_to, fsdp_to),
-            device_id_type=MESH,
-        ).start()
-
-    def hold(src, dst, number):
-        pltpu.make_async_copy(src, dst, sems.at[2 * number + 1]).start()
-
-    def await_all(buffer, number):
-        pltpu.make_async_copy(buffer, buffer, sems.at[2 * number + 1]).wait()
-
-    def tell_ids(step, carry):
-        send(ids_own, ids_all.at[chip, :, span], 4, lax.rem(ctx + step, ctx_count), member)
-        return carry
-
-    lax.fori_loop(1, ctx_count, tell_ids, 0)
 
     lane = lax.broadcasted_iota(jnp.int32, (blocks, 128), 1)
     loads[4].wait()
@@ -205,6 +179,46 @@
                 picked = jnp.where(lane // 16 == m, take_lanes(source[m], index), picked)
             scl[tile * 8 + n] = picked
 
+    pl.semaphore_wait(barrier, total - 1)
+
+    def pair_copy(src, dst, number, device):
+        copy = pltpu.make_async_remote_copy(
+            src_ref=src, dst_ref=dst, send_sem=pair_send.at[number],
+            recv_sem=pair_recv.at[number], device_id=device, device_id_type=MESH,
+        )
+        copy.start()
+        return copy
+
+    across = (sibling, member)
+    beside = (ctx, partner)
+    span = pl.ds(mine_at, rows)
+    near = xn.at[span, pl.ds(pl.multiple_of(member * depth, 128), depth)]
+    far = xn.at[span, pl.ds(pl.multiple_of(partner * depth, 128), depth)]
+    copy_x = pair_copy(near, near, 0, across)
+    copy_x_rest = pair_copy(far, far, 1, across)
+    copy_do = pair_copy(
+        do_ref.at[:, pl.ds(other_columns, half_columns)], do_all.at[span], 2, across
+    )
+
+    def send(src, dst, number, ctx_to, fsdp_to):
+        pltpu.make_async_remote_copy(
+            src_ref=src, dst_ref=dst, send_sem=sems.at[2 * number],
+            recv_sem=sems.at[2 * number + 1], device_id=(ctx_to, fsdp_to),
+            device_id_type=MESH,
+        ).start()
+
+    def hold(src, dst, number):
+        pltpu.make_async_copy(src, dst, sems.at[2 * number + 1]).start()
+
+    def await_all(buffer, number):
+        pltpu.make_async_copy(buffer, buffer, sems.at[2 * number + 1]).wait()
+
+    def tell_ids(step, carry):
+        send(ids_own, ids_all.at[chip, :, span], 4, lax.rem(ctx + step, ctx_count), member)
+        return carry
+
+    lax.fori_loop(1, ctx_count, tell_ids, 0)
+
     at = lax.broadcasted_iota(jnp.int32, (64, tokens), 0)
     feature = (8 * (at % 8) + at // 8).astype(F32)
     position = (lax.broadcasted_iota(jnp.int32, (64, tokens), 1) + chip * tokens).astype(F32)
@@ -227,7 +241,7 @@
     for code, level in enumerate(NF4_LEVELS):
         table = jnp.where(short_lane % 16 == code, F32(level), table)
 
-    def phase(paired, tile, half):
+    def phase(paired, tile, half, ready=None):
         if paired:
             shift = 16 + 96 * core
 
@@ -258,13 +272,15 @@
             vscl[n] = jnp.where(
                 chosen(half_lane), scale[:half_blocks], pltpu.roll(scale[half_blocks:], shift, 1)
             )
-        acc[...] = jnp.zeros_like(acc)
+        if ready is None:
+            acc[...] = jnp.zeros_like(acc)
         first = chosen(short_lane)
 
         def step(k, carry):
-            at = pl.multiple_of(member * depth + k * chunk, 128)
-            lower = xn[:, pl.ds(at, chunk)]
-            upper = xn[:, pl.ds(pl.multiple_of(at + half_depth, 128), chunk)]
+            if ready is None:
+                at = pl.multiple_of(member * depth + k * chunk, 128)
+                lower = xn[:, pl.ds(at, chunk)]
+                upper = xn[:, pl.ds(pl.multiple_of(at + half_depth, 128), chunk)]
             low_words, high_words, full_words = [], [], []
             for b in range(per_chunk):
                 row = pl.multiple_of(k * chunk + b * block_rows, block_rows)
@@ -300,18 +316,27 @@
                     planes.append(jnp.concatenate(pieces, axis=0))
                 weight = jnp.concatenate(planes, axis=1)
                 columns = slice(pair * 256, (pair + 1) * 256)
-                acc[0, :, columns] += dot(lower, weight)
-                acc[1, :, columns] += dot(upper, weight)
+                if ready is None:
+                    acc[0, :, columns] += dot(lower, weight)
+                    acc[1, :, columns] += dot(upper, weight)
+                else:
+                    weights[pl.ds(pl.multiple_of(k * chunk, chunk), chunk), columns] = weight
             return carry
 
         lax.fori_loop(0, half_depth // chunk, step, 0)
+        if ready is not None:
+            ready()
+            for side in range(2):
+                at = pl.multiple_of(member * depth + side * half_depth, 128)
+                for pair in range(4):
+                    columns = slice(pair * 256, (pair + 1) * 256)
+                    acc[side, :, columns] = dot(xn[:, pl.ds(at, half_depth)], weights[:, columns])
         keep = chosen(long_lane)
         for n in range(8):
             columns = slice(n * 128, (n + 1) * 128)
             acct[n] = jnp.where(keep, acc[0, :, columns], acc[1, :, columns]).T
 
     loads[6].wait()
-    copy_x.wait()
 
     def kv_field(group, part):
         at = pl.multiple_of(64 * group, 64) + 32 * part
@@ -319,7 +344,7 @@
             :, pl.ds(pl.multiple_of(at + 16, 16), 16), :
         ]
 
-    phase(True, 0, 0)
+    phase(True, 0, 0, copy_x.wait)
     copy_kv = [None, None]
     for part in (1, 0):
         send_kv[part] = kv_field(partner, part).astype(BF16)
@@ -371,9 +396,9 @@
         half = kv_all.at[block, part]
         pltpu.make_async_copy(half, half, block_recv.at[2 * block + part]).wait()
 
-    def relay(ahead):
+    def relay(ahead, parts=(0, 1)):
         block = 2 * (outer - 1 - ahead) + inner
-        for part in range(2):
+        for part in parts:
             await_block(block, part)
 
             @pl.when(has_next)
@@ -406,6 +431,10 @@
     @pl.when(outer > 0)
     def _():
         relay(0)
+
+    @pl.when(outer > 1)
+    def _():
+        relay(1, (0,))
 
     copy_q.wait()
     for head in range(heads):
@@ -416,6 +445,10 @@
         query = query + recv_q[:, 16 * head : 16 * head + 16, :].astype(F32)
         query = query + ADAPTER_SCALE * adapter
         queries[:128, columns] = rotate(query).reshape(128, tokens).astype(BF16)
+
+    @pl.when(outer > 1)
+    def _():
+        relay(1, (1,))
 
     soft_scale = 1.0 / math.sqrt(HEAD_SIZE)
     log_scale = soft_scale / math.log(2.0)
@@ -470,9 +503,9 @@
     def visit(step, carry):
         place = step - inner
         odd = lax.rem(place + 2, 2) == 1
-        ahead = (place + 1) // 2
-
-        @pl.when(odd & (ahead > 0) & (ahead < outer))
+        ahead = step // 2 + 1
+
+        @pl.when((lax.rem(step, 2) == 0) & (ahead > 1) & (ahead < outer))
         def _():
             relay(ahead)
 
@@ -510,27 +543,25 @@
         for number, device in enumerate(((ctx, partner), (sibling, partner), (sibling, member)))
     ]
 
-    up_pieces = up_part.shape[0]
-    up_stride = chips // up_pieces
-    up_mine = chip // up_stride
-    owner = lax.rem(chip, up_stride) == 0
-    up_slot = core * up_pieces + up_mine
-    ga_slot = quarter * up_pieces + up_mine
-    low = chip < chips // 2
-
-    def far_first(step, count):
-        return jnp.where(low, count - 1 - step, step)
-
+    owners, per = up_part.shape[:2]
+    stride = chips // 2 // owners
+    first_owner = chips // 4
+    turn = chip - first_owner
+    mine = turn // stride
+    owner = (turn >= 0) & (turn < owners * stride) & (lax.rem(turn + chips, stride) == 0)
+    up_slot = core * owners + mine
+    ga_slot = quarter * owners + mine
     back = 16 * (pd % 8) + pd // 8
     for head in range(heads):
         up = take_lanes(ADAPTER_SCALE * nt(lr_t, lin[head]), back[:16])
-        up_part[2 * head] = up[:8]
-        up_part[2 * head + 1] = up[8:]
+        for part in range(2):
+            piece = 2 * head + part
+            up_part[piece // per, piece % per] = up[8 * part : 8 * part + 8]
 
     def scatter(part, into, number):
         def one(step, carry):
-            j = far_first(step, up_pieces)
-            to = j * up_stride
+            j = far_first(step, owners)
+            to = first_owner + j * stride
 
             @pl.when(to != chip)
             def _():
@@ -538,11 +569,11 @@
 
             return carry
 
-        lax.fori_loop(0, up_pieces, one, 0)
+        lax.fori_loop(0, owners, one, 0)
 
         @pl.when(owner)
         def _():
-            hold(part.at[up_mine], into.at[chip], number)
+            hold(part.at[mine], into.at[chip], number)
 
     scatter(up_part, up_in, 0)
 
@@ -555,10 +586,10 @@
         copy.wait()
     middle = mid_own[...] + mid_in[0] + mid_in[1] + mid_in[2]
     middle = (ADAPTER_SCALE * middle).astype(BF16)
-    share = up_pieces * 128
+    share = owners * per * 128
     ga = dot(middle, xn[:, pl.ds(pl.multiple_of(quarter * share, 128), share)])
-    for j in range(up_pieces):
-        ga_part[j] = ga[:, j * 128 : (j + 1) * 128].astype(BF16)
+    for j in range(owners * per):
+        ga_part[j // per, j % per] = ga[:, j * 128 : (j + 1) * 128].astype(BF16)
     scatter(ga_part, ga_in, 1)
 
     copy_out = pair_copy(out_stage.at[pl.ds(other_at, rows)], out_in, 5, across)
@@ -601,12 +632,12 @@
     out_ref[:, pl.ds(other_columns, half_columns)] = out_in[...]
 
     await_all(up_all, 2)
-    for j in range(2 * up_pieces):
+    for j in range(2 * owners * per):
         row, col = 8 * (j % 2), 128 * (j // 2)
-        up_out[row : row + 8, col : col + 128] = up_all[j]
+        up_out[row : row + 8, col : col + 128] = up_all[j // per, j % per]
     await_all(ga_all, 3)
-    for j in range(4 * up_pieces):
-        ga_out[:, j * 128 : (j + 1) * 128] = ga_all[j].astype(F32)
+    for j in range(4 * owners * per):
+        ga_out[:, j * 128 : (j + 1) * 128] = ga_all[j // per, j % per].astype(F32)
 
     def drain(buffer, semaphore, sent):
         def one(step, carry):
@@ -618,7 +649,7 @@
     onward = has_next.astype(jnp.int32)
     passed = 2 * (onward + 1 - inner + outer * (onward + 1))
     drain(kv_all.at[chip, 0], block_send.at[0], passed)
-    scattered = up_pieces - owner.astype(jnp.int32)
+    scattered = owners - owner.astype(jnp.int32)
     drain(up_part.at[0], sems.at[0], scattered)
     drain(ga_part.at[0], sems.at[2], scattered)
     drain(up_sum, sems.at[4], jnp.where(owner, ctx_count - 1, 0))
@@ -653,7 +684,8 @@
     blocks = column_scale_quantized.shape[0]
     rank, local_columns = query_up_map.shape
     heads = local_columns // HEAD_SIZE // 2
-    up_pieces = 2 * heads
+    owners = math.gcd(2 * heads, chips // 2)
+    per = 2 * heads // owners
     vmem, dma = pltpu.VMEM, pltpu.SemaphoreType.DMA
     attn, ga, up = pl.pallas_call(
         functools.partial(step_kernel, counts),
@@ -676,6 +708,7 @@
             vmem(output_cotangent.shape, BF16),
             vmem((24, blocks, 128), F32),
             vmem((8, blocks // 2, 128), F32),
+            vmem((codes.shape[0] // 2, 1024), BF16),
             vmem((2, tokens, 1024), F32),
             vmem((8, 128, tokens), F32),
             vmem((tokens, width), BF16),
@@ -706,15 +739,15 @@
             vmem((rows, heads * 128), BF16),
             vmem((rank, tokens), F32),
             vmem((3, rank, tokens), F32),
-            vmem((up_pieces, rank, 128), BF16),
-            vmem((chips, rank, 128), BF16),
-            vmem((rank, 128), BF16),
-            vmem((4 * up_pieces, rank, 128), BF16),
-            vmem((up_pieces, 8, 128), F32),
-            vmem((chips, 8, 128), F32),
-            vmem((8, 128), F32),
-            vmem((2 * up_pieces, 8, 128), F32),
-            dma((9,)),
+            vmem((owners, per, rank, 128), BF16),
+            vmem((chips, per, rank, 128), BF16),
+            vmem((per, rank, 128), BF16),
+            vmem((4 * owners, per, rank, 128), BF16),
+            vmem((owners, per, 8, 128), F32),
+            vmem((chips, per, 8, 128), F32),
+            vmem((per, 8, 128), F32),
+            vmem((2 * owners, per, 8, 128), F32),
+            dma((10,)),
             dma((10,)),
             dma((10,)),
             dma((1,)),

time: 47.8 us -> 45.8 us (0.958)
  Pallas kernels: 47 us -> 45 us
    pallas_call x1, Pallas kernels: 46.2 us -> 44.1 us  [on_device(): pl.pallas_call(functools.partial(step_kernel, counts), out_shape=(vmem(ou...]
where the time goes in v5:
time: 45.8 us; the launch traced here: 45.6 us
  Pallas kernels  45 us (98%)
  between operations  0.64 us (1%)
    pallas_call x1, Pallas kernels, on_device(): pl.pallas_call(functools.partial(step_kernel, counts), out_shape=(vmem(ou...  44.1 us

profile of v5, /device:TPU:0, one launch (start us, length us, event | category | flops | bytes accessed | tf_op | source)
XLA Modules:
  0.0 45.6 jit_solution(3503372584535860472)
XLA Ops:
  0.6 44.1 %step.1 = (bf16[128,1024]{1,0:T(8,128)(2,1)S(1)}, f32[16,4096]{1,0:T(8,128)S(1)}, f32[16,1024]{1,0:T(8,128)S(1)}) custom-call(bf16[128,4096]{1,0:T(8,128)(2,1)} %x_hbm.1, f32[1,4096]{1,0:T(1,128)} %bitcast.6, s32[2048,384]{1,0:T(8,128)} %codes_hbm.1, s32[32,3072]{1,0:T(8,128)} %cs_hbm.1, f32[1,64]{1,0:T(1,128)} %bitcast.7, bf16[16,4096]{1,0:T(8,128)(2,1)} %bitcast.5, ...), custom_call_target="tpu_custom_call" | custom-call | tf_op jit(solution)/shard_map/step/pallas_call | solution.py:690
  44.8 0.8 %store.1 = (bf16[128,1024]{1,0:T(8,128)(2,1)}, f32[16,4096]{1,0:T(8,128)}, f32[16,1024]{1,0:T(8,128)}) custom-call(bf16[128,1024]{1,0:T(8,128)(2,1)S(1)} %get-tuple-element.9.attn_ref, f32[16,4096]{1,0:T(8,128)S(1)} %get-tuple-element.10.ga_ref, f32[16,1024]{1,0:T(8,128)S(1)} %get-tuple-element.11.up_ref), custom_call_target="tpu_custom_call" | custom-call | tf_op jit(solution)/shard_map/store/pallas_call | solution.py:765

commit v6 on v5

--- a/solution.py
+++ b/solution.py
@@ -218,13 +218,6 @@
         return carry
 
     lax.fori_loop(1, ctx_count, tell_ids, 0)
-
-    at = lax.broadcasted_iota(jnp.int32, (64, tokens), 0)
-    feature = (8 * (at % 8) + at // 8).astype(F32)
-    position = (lax.broadcasted_iota(jnp.int32, (64, tokens), 1) + chip * tokens).astype(F32)
-    angle = position * jnp.exp(feature * (-2.0 * math.log(ROPE_BASE) / HEAD_SIZE))
-    cos_ref[...] = jnp.cos(angle)
-    sin_ref[...] = jnp.sin(angle)
 
     pr = lax.broadcasted_iota(jnp.int32, (128, 128), 0)
     pd = lax.broadcasted_iota(jnp.int32, (128, 128), 1)
@@ -357,6 +350,13 @@
     send_q[...] = (acct[:, :64, :] + acct[:, 64:, :]).astype(BF16)
     copy_q = pair_copy(send_q, recv_q, 4, beside)
 
+    at = lax.broadcasted_iota(jnp.int32, (64, tokens), 0)
+    feature = (8 * (at % 8) + at // 8).astype(F32)
+    position = (lax.broadcasted_iota(jnp.int32, (64, tokens), 1) + chip * tokens).astype(F32)
+    angle = position * jnp.exp(feature * (-2.0 * math.log(ROPE_BASE) / HEAD_SIZE))
+    cos_ref[...] = jnp.cos(angle)
+    sin_ref[...] = jnp.sin(angle)
+
     loads[7].wait()
     loads[8].wait()
     copy_x_rest.wait()
@@ -424,13 +424,13 @@
         def _():
             send_block(chip, 1 - part, chip + 1)
 
+    @pl.when(outer > 0)
+    def _():
+        relay(0)
+
     place = 3 * member + core
     phase(False, place // 2, lax.rem(place, 2))
     own_q[...] = acct[:, :64, :] + acct[:, 64:, :]
-
-    @pl.when(outer > 0)
-    def _():
-        relay(0)
 
     @pl.when(outer > 1)
     def _():

time: 45.8 us -> 45.5 us (level)
  no operation moved by 1% of the time
where the time goes in v6:
time: 45.5 us; the launch traced here: 45.3 us
  Pallas kernels  44.7 us (98%)
  between operations  0.64 us (1%)
    pallas_call x1, Pallas kernels, on_device(): pl.pallas_call(functools.partial(step_kernel, counts), out_shape=(vmem(ou...  43.8 us

profile of v6, /device:TPU:0, one launch (start us, length us, event | category | flops | bytes accessed | tf_op | source)
XLA Modules:
  0.0 45.3 jit_solution(6995324379106492699)
XLA Ops:
  0.6 43.8 %step.1 = (bf16[128,1024]{1,0:T(8,128)(2,1)S(1)}, f32[16,4096]{1,0:T(8,128)S(1)}, f32[16,1024]{1,0:T(8,128)S(1)}) custom-call(bf16[128,4096]{1,0:T(8,128)(2,1)} %x_hbm.1, f32[1,4096]{1,0:T(1,128)} %bitcast.6, s32[2048,384]{1,0:T(8,128)} %codes_hbm.1, s32[32,3072]{1,0:T(8,128)} %cs_hbm.1, f32[1,64]{1,0:T(1,128)} %bitcast.7, bf16[16,4096]{1,0:T(8,128)(2,1)} %bitcast.5, ...), custom_call_target="tpu_custom_call" | custom-call | tf_op jit(solution)/shard_map/step/pallas_call | solution.py:690
  44.5 0.8 %store.1 = (bf16[128,1024]{1,0:T(8,128)(2,1)}, f32[16,4096]{1,0:T(8,128)}, f32[16,1024]{1,0:T(8,128)}) custom-call(bf16[128,1024]{1,0:T(8,128)(2,1)S(1)} %get-tuple-element.9.attn_ref, f32[16,4096]{1,0:T(8,128)S(1)} %get-tuple-element.10.ga_ref, f32[16,1024]{1,0:T(8,128)S(1)} %get-tuple-element.11.up_ref), custom_call_target="tpu_custom_call" | custom-call | tf_op jit(solution)/shard_map/store/pallas_call | solution.py:765
